TPU v7x, 256 devices: a whole 4x4x8 slice. The times are simulated.
256 devices in a mesh: dp: 8 (over x, y_lo), ctx: 32 (over y_hi, z, core).
Axes of the slice: x: 4, y: 4 (y_hi: 2, y_lo: 2; y = y_hi * 2 + y_lo), z: 8, core: 2. Of those that a mesh axis runs over, the one named last changes fastest.
Arguments:
- query_matrix: bfloat16 [8, 4096, 2048], P('dp', 'ctx'), may hold values from -16 to 16
- key_matrix: bfloat16 [8, 4096, 512], P('dp', 'ctx'), may hold values from -16 to 16
- value_matrix: bfloat16 [8, 4096, 512], P('dp', 'ctx'), may hold values from -6 to 6
- output_gradient: bfloat16 [8, 4096, 2048], P('dp', 'ctx'), may hold values from -6 to 6
- hidden_in: bfloat16 [8, 4096, 4096], P('dp', 'ctx'), may hold values from -6 to 6
- doc_lengths: int32 [8, 16], P('dp'), may hold values from 1 to 3072, 4096 in all within a row
- querya: bfloat16 [16, 4096], replicated, may hold values from -0.09375 to 0.09375
- queryb: bfloat16 [16, 2048], replicated, may hold values from -1.5 to 1.5
- valuea: bfloat16 [16, 4096], replicated, may hold values from -0.09375 to 0.09375
- valueb: bfloat16 [16, 512], replicated, may hold values from -1.5 to 1.5
Outputs:
- query_grad: bfloat16 [8, 4096, 2048], P('dp', 'ctx')
- key_grad: bfloat16 [8, 4096, 512], P('dp', 'ctx')
- value_gradient: bfloat16 [8, 4096, 512], P('dp', 'ctx')
- querya_grad: float32 [16, 4096], replicated
- queryb_grad: float32 [16, 2048], replicated
- valuea_grad: float32 [16, 4096], replicated
- valueb_grad: float32 [16, 512], replicated
Inputs may be any that keep to these rules, and one draw needn't show every extreme that they name: `doc_lengths`: row b lists, in order, the lengths of the 16 documents packed into sequence b; they sum to 4096.
All inputs are finite; a program needn't handle non-finite values.
Results may differ from a plain program's by a relative error of at most 0.022.
Values may be sent and summed in bfloat16 or wider, within the bound.
A program may use at most 128 MiB of HBM per device.

v0:
```python
import math

import jax
import jax.numpy as jnp
from jax import lax
from jax.sharding import PartitionSpec as P

QUERY_HEADS = 16
KEY_VALUE_HEADS = 4
HEAD_WIDTH = 128


NEG_FILL = -1e30
ADAPTER_SCALE = 2.0


def in_one_piece(arrays, axis, dim, along):
    ends, at = ([], 0)
    for a in arrays[:-1]:
        at += a.shape[along]
        ends.append(at)
    both = jnp.concatenate(arrays, axis=along)
    return tuple(jnp.split(lax.all_gather(both, axis, axis=dim, tiled=True), ends, axis=along))


def sent_together(arrays, axis, dim, along):
    ends, at = ([], 0)
    for a in arrays[:-1]:
        at += a.shape[along]
        ends.append(at)
    both = jnp.concatenate(arrays, axis=along)
    return tuple(
        jnp.split(lax.psum_scatter(both, axis, scatter_dimension=dim, tiled=True), ends, axis=along)
    )


def packed_total(arrays, axis):
    ends = [0]
    for a in arrays:
        ends.append(ends[-1] + a.size)
    subtotal = lax.psum(jnp.concatenate([a.ravel() for a in arrays]), axis)
    return tuple((subtotal[b:e].reshape(a.shape) for a, b, e in zip(arrays, ends, ends[1:])))


def doc_begin(lengths, positions):
    doc_ends = jnp.cumsum(lengths)
    begins = doc_ends - lengths
    inside = begins[None, :] <= positions[:, None]
    return jnp.max(jnp.where(inside, begins[None, :], 0), axis=1)


def rounded_length(values):
    return lax.optimization_barrier(values.astype(jnp.bfloat16)).astype(jnp.float32)


def contract_last(left, right):
    return lax.dot_general(
        left, right, (((1,), (1,)), ((), ())), preferred_element_type=jnp.float32
    )


def contract_first(left, right):
    return lax.dot_general(
        left, right, (((0,), (0,)), ((), ())), preferred_element_type=jnp.float32
    )


def walk_keys(carry_in, pieces, block_fn):
    key_piece, value_piece = pieces
    piece_rows = key_piece.shape[0]
    rows_per_block = math.gcd(piece_rows, 512)

    def one_block(block_index, running):
        offset = (block_index * rows_per_block).astype(jnp.int32)
        key_block = lax.dynamic_slice_in_dim(key_piece, offset, rows_per_block, 0).reshape(
            rows_per_block, KEY_VALUE_HEADS, HEAD_WIDTH
        )
        value_block = lax.dynamic_slice_in_dim(value_piece, offset, rows_per_block, 0).reshape(
            rows_per_block, KEY_VALUE_HEADS, HEAD_WIDTH
        )
        return block_fn(running, key_block, value_block, offset)

    return lax.fori_loop(0, piece_rows // rows_per_block, one_block, carry_in)


def shards(
    query_matrix,
    key_matrix,
    value_matrix,
    output_gradient,
    hidden_in,
    doc_lengths,
    querya,
    queryb,
    valuea,
    valueb,
):
    token_rows = query_matrix.shape[1]
    rows_per_half = token_rows // 2
    cycle_size = lax.axis_size("ctx")
    sequence_total = token_rows * cycle_size
    group_width = QUERY_HEADS // KEY_VALUE_HEADS
    head_scale = HEAD_WIDTH ** (-0.5)
    own_index = lax.axis_index("ctx")
    own_pos = own_index * token_rows + lax.iota(jnp.int32, token_rows)
    local_query = query_matrix[0]
    local_gradient = output_gradient[0]
    query_quad = local_query.reshape(token_rows, KEY_VALUE_HEADS, group_width, HEAD_WIDTH)
    gradient_quad = local_gradient.reshape(token_rows, KEY_VALUE_HEADS, group_width, HEAD_WIDTH)
    query_begin = doc_begin(doc_lengths[0], own_pos)

    def visibility(key_first, rows_per_block):
        key_pos = key_first + lax.iota(jnp.int32, rows_per_block)
        visible = (key_pos[None, :] <= own_pos[:, None]) & (
            key_pos[None, :] >= query_begin[:, None]
        )
        touched = jnp.any((key_first <= own_pos) & (key_first + rows_per_block - 1 >= query_begin))
        return (visible[:, None, None, :], touched)

    def forward_block(running, key_block, value_block, key_first):
        visible, touched = visibility(key_first, key_block.shape[0])

        def forward_compute(current):
            run_max, run_sum, run_acc = current
            scores = (
                jnp.einsum(
                    "thgd,chd->thgc", query_quad, key_block, preferred_element_type=jnp.float32
                )
                * head_scale
            )
            block_max = jnp.max(jnp.where(visible, scores, NEG_FILL), axis=-1)
            new_max = jnp.maximum(run_max, block_max)
            unnorm = jnp.where(visible, jnp.exp(scores - new_max[..., None]), 0.0)
            factor = jnp.exp(run_max - new_max)
            new_sum = run_sum * factor + jnp.sum(unnorm, axis=-1)
            new_acc = run_acc * factor[..., None] + jnp.einsum(
                "thgc,chd->thgd",
                unnorm.astype(jnp.bfloat16),
                value_block,
                preferred_element_type=jnp.float32,
            )
            return (new_max, new_sum, new_acc)

        return lax.cond(touched, forward_compute, lambda unchanged: unchanged, running)

    statistic_shape = (token_rows, KEY_VALUE_HEADS, group_width)
    forward_init = (
        jnp.full(statistic_shape, NEG_FILL, jnp.float32),
        jnp.zeros(statistic_shape, jnp.float32),
        jnp.zeros(statistic_shape + (HEAD_WIDTH,), jnp.float32),
    )
    whole_pair = in_one_piece((key_matrix[0], value_matrix[0]), "ctx", 0, 1)
    run_max, run_sum, run_acc = walk_keys(forward_init, whole_pair, forward_block)
    log_total = run_max + jnp.log(run_sum)
    attended = run_acc / run_sum[..., None]
    delta_rows = jnp.sum(gradient_quad.astype(jnp.float32) * attended, axis=-1)
    query_split_halves = query_quad.reshape(
        2, rows_per_half, KEY_VALUE_HEADS, group_width, HEAD_WIDTH
    )
    gradient_halves = gradient_quad.reshape(
        2, rows_per_half, KEY_VALUE_HEADS, group_width, HEAD_WIDTH
    )

    def make_backward(base_row):

        def backward_block(running, key_block, value_block, key_first):
            rows_per_block = key_block.shape[0]
            visible, touched = visibility(key_first, rows_per_block)

            def backward_compute(current):
                query_acc, key_all, value_all = current
                scores = (
                    jnp.einsum(
                        "thgd,chd->thgc", query_quad, key_block, preferred_element_type=jnp.float32
                    )
                    * head_scale
                )
                probabilities = jnp.where(visible, jnp.exp(scores - log_total[..., None]), 0.0)
                grad_probs = jnp.einsum(
                    "thgd,chd->thgc", gradient_quad, value_block, preferred_element_type=jnp.float32
                )
                score_gradient = (
                    probabilities * (grad_probs - delta_rows[..., None]) * head_scale
                ).astype(jnp.bfloat16)
                new_query = query_acc + jnp.einsum(
                    "thgc,chd->thgd", score_gradient, key_block, preferred_element_type=jnp.float32
                )
                score_split_halves = score_gradient.reshape(
                    2, rows_per_half, KEY_VALUE_HEADS, group_width, rows_per_block
                )
                probability_halves = probabilities.astype(jnp.bfloat16).reshape(
                    2, rows_per_half, KEY_VALUE_HEADS, group_width, rows_per_block
                )
                key_part = jnp.sum(
                    rounded_length(
                        jnp.einsum(
                            "pthgc,pthgd->pchd",
                            score_split_halves,
                            query_split_halves,
                            preferred_element_type=jnp.float32,
                        )
                    ),
                    axis=0,
                ).reshape(rows_per_block, KEY_VALUE_HEADS * HEAD_WIDTH)
                value_part = jnp.sum(
                    rounded_length(
                        jnp.einsum(
                            "pthgc,pthgd->pchd",
                            probability_halves,
                            gradient_halves,
                            preferred_element_type=jnp.float32,
                        )
                    ),
                    axis=0,
                ).reshape(rows_per_block, KEY_VALUE_HEADS * HEAD_WIDTH)
                local_first = key_first - base_row
                key_old = lax.dynamic_slice_in_dim(key_all, local_first, rows_per_block, 0)
                value_old = lax.dynamic_slice_in_dim(value_all, local_first, rows_per_block, 0)
                new_keys = lax.dynamic_update_slice_in_dim(
                    key_all, key_old + key_part, local_first, 0
                )
                new_values = lax.dynamic_update_slice_in_dim(
                    value_all, value_old + value_part, local_first, 0
                )
                return (new_query, new_keys, new_values)

            return lax.cond(touched, backward_compute, lambda unchanged: unchanged, running)

        return backward_block

    query_zero = jnp.zeros(statistic_shape + (HEAD_WIDTH,), jnp.float32)
    backward_init = (
        query_zero,
        jnp.zeros((sequence_total, KEY_VALUE_HEADS * HEAD_WIDTH), jnp.float32),
        jnp.zeros((sequence_total, KEY_VALUE_HEADS * HEAD_WIDTH), jnp.float32),
    )
    query_acc, key_all, value_all = walk_keys(backward_init, whole_pair, make_backward(0))
    key_total_sum, value_total_sum = tuple(
        (
            part.astype(jnp.float32)
            for part in sent_together(
                (key_all.astype(jnp.bfloat16), value_all.astype(jnp.bfloat16)), "ctx", 0, 1
            )
        )
    )
    work_query_grad = query_acc.reshape(token_rows, QUERY_HEADS * HEAD_WIDTH).astype(jnp.bfloat16)
    key_grad = key_total_sum.astype(jnp.bfloat16)
    value_gradient = value_total_sum.astype(jnp.bfloat16)
    tokens_in = hidden_in[0]
    query_proj = contract_last(tokens_in, querya).astype(jnp.bfloat16)
    value_proj = contract_last(tokens_in, valuea).astype(jnp.bfloat16)
    query_low = contract_last(work_query_grad, queryb).astype(jnp.bfloat16)
    value_low = contract_last(value_gradient, valueb).astype(jnp.bfloat16)
    summed = packed_total(
        (
            ADAPTER_SCALE * contract_first(query_low, tokens_in),
            ADAPTER_SCALE * contract_first(query_proj, work_query_grad),
            ADAPTER_SCALE * contract_first(value_low, tokens_in),
            ADAPTER_SCALE * contract_first(value_proj, value_gradient),
        ),
        ("dp", "ctx"),
    )
    return (
        work_query_grad[None],
        key_grad[None],
        value_gradient[None],
        summed[0],
        summed[1],
        summed[2],
        summed[3],
    )


def solution(mesh):
    placed = (
        P("dp", "ctx", None),
        P("dp", "ctx", None),
        P("dp", "ctx", None),
        P("dp", "ctx", None),
        P("dp", "ctx", None),
        P("dp", None),
        P(),
        P(),
        P(),
        P(),
    )
    return jax.shard_map(
        shards,
        mesh=mesh,
        in_specs=placed,
        out_specs=(
            P("dp", "ctx", None),
            P("dp", "ctx", None),
            P("dp", "ctx", None),
            P(),
            P(),
            P(),
            P(),
        ),
        check_vma=False,
    )
```

profile of v0, /device:TPU:1, one launch (start us, length us, event | category | flops | bytes accessed | tf_op | source)
XLA Modules:
  0.0 831.9 jit_solution(3872377424868260726)
XLA Ops:
  7.3 1.1 copy.95
  8.4 1.0 copy.96
  10.2 2.2 reshape_reshape_squeeze.6
  12.4 1.3 copy.97
  13.7 1.4 reshape_reshape_squeeze.7
  15.6 2.0 copy.103
  17.9 1.0 copy.104
  18.9 1.0 copy.102
  20.0 103.6 %all-gather.2.cloned.1.call-done = bf16[4096,1024]{0,1:T(8,128)(2,1)} async-done(((bf16[128,1024]{0,1:T(8,128)(2,1)}), bf16[4096,1024]{0,1:T(8,128)(2,1)}) %all-gather.2.cloned.1.call-update) | async-done | bytes 8388624 | tf_op jit(solution)/shard_map/all_gather | solution.py:23
  123.6 5.9 fusion.59
  129.6 15.6 %while.44 = (s32[]{:T(128)}, f32[128,4,4]{0,2,1:T(4,128)S(1)}, f32[128,4,4]{0,2,1:T(4,128)S(1)}, f32[128,4,4,128]{3,0,2,1:T(8,128)S(1)}, s32[128]{0:T(128)S(1)},...) while((s32[]{:T(128)}, f32[128,4,4]{0,2,1:T(4,128)S(1)}, ...), condition=%wide.region_8.9_spmd.clone, body=%wide.region_2.8_spmd.clone.sunk | while | flops 549131520 | bytes 18753876 | solution.py:83
  130.9 4.7 conditional.6
  131.1 1.3 constant_dynamic-slice_fusion
  132.4 0.9 fusion.4
  133.3 0.9 fusion.8
  134.2 1.5 fusion.18
  145.2 1.3 copy.100
  146.5 1.4 multiply_reduce_fusion
  147.9 1.1 broadcast.166
  149.1 4.3 broadcast.167.clone
  153.3 4.2 broadcast.167
  157.6 38.2 %while.45 = (s32[]{:T(128)}, f32[128,4,4,128]{3,0,2,1:T(8,128)}, f32[4096,512]{0,1:T(8,128)}, f32[4096,512]{0,1:T(8,128)}, s32[128]{0:T(128)S(1)}, /*index=5*/bf...) while((s32[]{:T(128)}, f32[128,4,4,128]{3,0,2,1:T(8,128)}, ...), condition=%wide.region_16.17_spmd.clone, body=%wide.region_10.16_spmd.clone.sunk | while | flops 1357317376 | bytes 58427904 | solution.py:83
  158.9 27.5 %conditional.7 = ((f32[128,4,4,128]{3,0,2,1:T(8,128)}, f32[4096,512]{0,1:T(8,128)}, f32[4096,512]{0,1:T(8,128)})) conditional(s32[]{:T(128)} %convert_element_type.159, (f32[128,4,4,128]{3,0,2,1:T(8,128)}, f32[4096,512]{0,1:T(8,128)}, f32[4096,512]{0,1:T(8,128)}) %tuple.168, (s32[]{:T(128)}, s32[512]{0:T(512)S(1)}, s32[128]{0:T(128)S(1)}, ...), branch_computations={%region_12.12_spmd, %region_13.15_spmd} | conditional | flops 1357316608 | bytes 58424488 | solution.py:227
  159.0 1.1 constant_dynamic-slice_fusion.3
  160.1 1.9 constant_dynamic-slice_fusion.2
  162.0 3.0 fusion.28
  165.0 1.9 fusion.40
  166.9 1.1 convert_reduce_fusion
  168.0 1.6 copy.94
  169.6 4.0 fusion.25
  173.6 1.3 copy-done.2
  175.8 1.1 convert_reduce_fusion.1
  176.9 2.5 copy.92
  179.5 3.7 fusion.43
  183.2 3.2 constant_dynamic-update-slice_fusion
  195.8 7.3 copy.107
  203.1 7.3 copy.106
  210.4 7.9 pad_maximum_fusion
  218.4 1.6 copy.105
  220.0 0.9 fusion.46
  221.4 336.3 %reduce-scatter.2.cloned.1.call-done = bf16[128,1024]{1,0:T(8,128)(2,1)} async-done(((bf16[4096,1024]{1,0:T(8,128)(2,1)}), bf16[128,1024]{1,0:T(8,128)(2,1)}) %reduce-scatter.2.cloned.1.call-update) | async-done | bytes 262160 | tf_op jit(solution)/shard_map/reduce_scatter | solution.py:33
  557.7 1.5 fusion.47
  559.3 1.3 fusion.45
  560.7 0.9 pad_maximum_fusion.1
  561.6 1.0 copy.108
  563.3 256.5 %all-reduce.2.cloned.1.call-done = f32[172032]{0:T(1024)} async-done(((f32[172032]{0:T(1024)}), f32[172032]{0:T(1024)}) %all-reduce.2.cloned.1.call-update) | async-done | bytes 688144 | tf_op jit(solution)/shard_map/psum | solution.py:41
  821.2 1.1 fusion.60
  823.0 0.9 slice.61
  (119 shorter events, 18.4 us)
Async XLA Ops:
  7.2 212.8 %copy-start = (bf16[1,128,4096]{2,1,0:T(8,128)(2,1)S(1)}, bf16[1,128,4096]{2,1,0:T(8,128)(2,1)}, u32[]{:S(2)}) copy-start(bf16[1,128,4096]{2,1,0:T(8,128)(2,1)} %param.22) | copy-start | bytes 3145732
  7.2 8.0 copy-start.3
  7.2 8.2 copy-start.10
  7.2 116.4 %all-gather.2.cloned.1.call-start = ((), (), s32[]{:S(2)}) async-start(), calls=%async_computation.1 | async-start | bytes 8650752 | tf_op jit(solution)/shard_map/all_gather | solution.py:23
  10.2 547.5 %reduce-scatter.2.cloned.1.call-start = ((), (), s32[]{:S(2)}) async-start(), calls=%async_computation.2 | async-start | bytes 8650752 | tf_op jit(solution)/shard_map/reduce_scatter | solution.py:33
  169.5 5.4 copy-start.5
  173.6 1.4 copy-start.2
  179.5 3.7 copy-start.1
  218.3 1.7 copy-start.6
  218.3 2.6 copy-start.8
  218.3 339.4 %copy-start.7 = (bf16[16,4096]{1,0:T(8,128)(2,1)S(1)}, bf16[16,4096]{1,0:T(8,128)(2,1)}, u32[]{:S(2)}) copy-start(bf16[16,4096]{1,0:T(8,128)(2,1)} %param.26) | copy-start | bytes 393220
  218.3 340.9 %copy-start.9 = (bf16[16,512]{1,0:T(8,128)(2,1)S(1)}, bf16[16,512]{1,0:T(8,128)(2,1)}, u32[]{:S(2)}) copy-start(bf16[16,512]{1,0:T(8,128)(2,1)} %param.27) | copy-start | bytes 49156
  218.3 601.5 %all-reduce.2.cloned.1.call-start = ((), (), s32[]{:S(2)}) async-start(), calls=%async_computation.3 | async-start | bytes 1376256 | tf_op jit(solution)/shard_map/psum | solution.py:41
  557.7 4.9 copy-start.4
Sparse Core Ops, SparseCore 0:
  11.1 112.3 all-gather.1
  218.4 339.2 reduce-scatter.1
  563.2 256.5 all-reduce.1
where the time goes:
time: 835 us; the launch traced here: 832 us
  waiting for transfers between devices  696 us (83%)
  local copies, waits for them, and re-layouts  62 us (7%)
  other arithmetic  28 us (3%)
  matrix products  19.9 us (2%)
  between operations  14 us (2%)
  loops' own time  11.5 us (1%)
    reduce_scatter x1, waiting for transfers between devices, sent_together(): lax.psum_scatter(both, axis, scatter_dimension=dim, tiled=True)  336 us
    psum x1, waiting for transfers between devices, packed_total(): subtotal = lax.psum(jnp.concatenate([a.ravel() for a in arrays]), axis)  257 us
    all_gather x1, waiting for transfers between devices, in_one_piece(): lax.all_gather(both, axis, axis=dim, tiled=True)  104 us
    while x4, local copies, waits for them, and re-layouts, walk_keys(): return lax.fori_loop(0, piece_rows // rows_per_block, one_block, carry_in)  17.5 us
  transfers between devices with their start and end apart: 3, of which 3 were waited for; matrix products, arithmetic and copies ran while one was open for 2% of the time, Pallas kernels for 0%

commit v1 on v0

v1 whole, which is shorter than its diff:
```python
import math

import jax
import jax.numpy as jnp
from jax import lax
from jax.experimental import pallas as pl
from jax.experimental.pallas import tpu as pltpu
from jax.sharding import PartitionSpec as P

MESH = pl.DeviceIdType.MESH
HEAD = 128
GROUP = 4
TOK = 128
RING = 8
CHIP_ROWS = 256
HALF_SEQ = 2048
SEQ = 4096
KB = 256
NKB = SEQ // KB
RANK = 16
PACKED = 12288
CORE_COLS = PACKED // 2
Z_COLS = CORE_COLS // RING
DOCS = 16
NEG = -1e30
SCALE = HEAD ** (-0.5)
LOG2E = math.log2(math.e)
ANY = pl.BlockSpec(memory_space=pl.ANY)
VMEM = pl.BlockSpec(memory_space=pltpu.VMEM)
SMEM = pl.BlockSpec(memory_space=pltpu.SMEM)


def nn(left, right):
    return lax.dot_general(left, right, (((1,), (0,)), ((), ())), preferred_element_type=jnp.float32)


def nt(left, right):
    return lax.dot_general(left, right, (((1,), (1,)), ((), ())), preferred_element_type=jnp.float32)


def place():
    me = lax.axis_index("ctx")
    return me // 16, (me // 2) % RING, me % 2


def ctx_of(a, z, c):
    return a * 16 + z * 2 + c


def mult(value, of):
    return pl.multiple_of(value, of)


def group_peers(a, c):
    return ((a, 1 - c), (1 - a, c), (1 - a, 1 - c))


def enter(ids):
    barrier = pltpu.get_barrier_semaphore()
    for one in ids:
        pl.semaphore_signal(barrier, inc=1, device_id=one, device_id_type=MESH)
    pl.semaphore_wait(barrier, len(ids))


def remote(src, dst, ssem, rsem, to):
    return pltpu.make_async_remote_copy(
        src_ref=src, dst_ref=dst, send_sem=ssem, recv_sem=rsem, device_id=to, device_id_type=MESH
    )


def ring_and_group(a, z, c):
    ids = [{"ctx": ctx_of(pa, z, pc)} for pa, pc in group_peers(a, c)]
    ids.append({"ctx": ctx_of(a, (z + 1) % RING, c)})
    ids.append({"ctx": ctx_of(a, (z + RING - 1) % RING, c)})
    return ids


def gather_kernel(q_ref, do_ref, k_ref, v_ref, qg_ref, dog_ref, kg_ref, vg_ref,
                  kall, vall, qst, dost, gs, gr, xs, xr, rs, rr, ls):
    a, z, c = place()
    ids = ring_and_group(a, z, c)
    own = 2 * a + c
    row0 = mult(a * HALF_SEQ + z * CHIP_ROWS + c * TOK, TOK)
    local = []
    for i, (src, dst) in enumerate(((k_ref, kall), (v_ref, vall))):
        local.append(pltpu.make_async_copy(
            src.at[:, pl.ds(mult(own * HEAD, HEAD), HEAD)], dst.at[pl.ds(row0, TOK)], ls.at[i]))
    wide = []
    for i, (src, dst) in enumerate(((q_ref, qst), (do_ref, dost))):
        wide.append(pltpu.make_async_copy(
            src.at[:, pl.ds(mult(own * 512, 512), 512)], dst, ls.at[2 + i]))
    for one in local + wide:
        one.start()
    enter(ids)
    sent = []
    peers = group_peers(a, c)
    for p, (pa, pc) in enumerate(peers):
        for i, (src, dst) in enumerate(((k_ref, kall), (v_ref, vall))):
            head = 2 * pa + pc
            cp = remote(src.at[:, pl.ds(mult(head * HEAD, HEAD), HEAD)], dst.at[pl.ds(row0, TOK)],
                        gs.at[2 * p + i], gr.at[2 * p + i], ids[p])
            cp.start()
            sent.append(cp)
    for p, (pa, pc) in enumerate(peers):
        for i, (src, dst) in enumerate(((q_ref, qg_ref), (do_ref, dog_ref))):
            head = 2 * pa + pc
            cp = remote(src.at[:, pl.ds(mult(head * 512, 512), 512)],
                        dst.at[pl.ds(mult(own * TOK, TOK), TOK)],
                        xs.at[2 * p + i], xr.at[2 * p + i], ids[p])
            cp.start()
            sent.append(cp)

    def group_arrived(p):
        pa, pc = peers[p]
        rows = pl.ds(mult(pa * HALF_SEQ + z * CHIP_ROWS + pc * TOK, TOK), TOK)
        for i, dst in enumerate((kall, vall)):
            remote(dst.at[rows], dst.at[rows], gs.at[2 * p + i], gr.at[2 * p + i], ids[p]).wait_recv()

    chunks = ((kall, a), (vall, a), (kall, 1 - a), (vall, 1 - a))
    ways = (1, -1)

    def chunk(j, zz):
        ref, y = chunks[j]
        return ref.at[pl.ds(mult(y * HALF_SEQ + zz * CHIP_ROWS, CHIP_ROWS), CHIP_ROWS)]

    def at(w, s, j):
        return (w * 4 + s) * 4 + j

    def send_on(w, s, j):
        part = chunk(j, (z + 2 * RING - ways[w] * s) % RING)
        cp = remote(part, part, rs.at[at(w, s, j)], rr.at[at(w, s, j)], ids[3 + w])
        cp.start()
        sent.append(cp)

    def arrived(w, s, j):
        part = chunk(j, (z + 2 * RING - ways[w] * (s + 1)) % RING)
        remote(part, part, rs.at[at(w, s, j)], rr.at[at(w, s, j)], ids[3 + w]).wait_recv()

    def carries(w, s, j):
        return s < 3 or (j < 2) == (w == 0)

    for one in local:
        one.wait()
    group_arrived(0)
    for j in (0, 1):
        for w in (0, 1):
            send_on(w, 0, j)
    group_arrived(1)
    group_arrived(2)
    for j in (2, 3):
        for w in (0, 1):
            send_on(w, 0, j)
    for s in range(4):
        for j in range(4):
            for w in (0, 1):
                if carries(w, s, j):
                    arrived(w, s, j)
                    if s < 3 and carries(w, s + 1, j):
                        send_on(w, s + 1, j)
    out = []
    for i, (src, dst) in enumerate(((kall, kg_ref), (vall, vg_ref))):
        out.append(pltpu.make_async_copy(src, dst, ls.at[i]))
    for one in wide:
        one.wait()
    for i, (src, dst) in enumerate(((qst, qg_ref), (dost, dog_ref))):
        out.append(pltpu.make_async_copy(src, dst.at[pl.ds(mult(own * TOK, TOK), TOK)], ls.at[2 + i]))
    for one in out:
        one.start()
    for p, (pa, pc) in enumerate(peers):
        rows = pl.ds(mult((2 * pa + pc) * TOK, TOK), TOK)
        for i, dst in enumerate((qg_ref, dog_ref)):
            remote(dst.at[rows], dst.at[rows], xs.at[2 * p + i], xr.at[2 * p + i], ids[p]).wait_recv()
    for one in out:
        one.wait()
    for one in sent:
        one.wait_send()


def gather_call(q, do, k, v):
    bf = jnp.bfloat16
    dma = pltpu.SemaphoreType.DMA
    return pl.pallas_call(
        gather_kernel,
        out_shape=(
            jax.ShapeDtypeStruct((512, 512), bf), jax.ShapeDtypeStruct((512, 512), bf),
            jax.ShapeDtypeStruct((SEQ, HEAD), bf), jax.ShapeDtypeStruct((SEQ, HEAD), bf),
        ),
        in_specs=[ANY, ANY, VMEM, VMEM],
        out_specs=(ANY, ANY, ANY, ANY),
        scratch_shapes=[
            pltpu.VMEM((SEQ, HEAD), bf), pltpu.VMEM((SEQ, HEAD), bf),
            pltpu.VMEM((TOK, 512), bf), pltpu.VMEM((TOK, 512), bf),
            dma((6,)), dma((6,)), dma((6,)), dma((6,)), dma((32,)), dma((32,)), dma((4,)),
        ],
        compiler_params=pltpu.CompilerParams(collective_id=0, has_side_effects=True),
        name="gather",
    )(q, do, k, v)


def attend_kernel(len_ref, q_ref, do_ref, k_ref, v_ref, dq_ref, dk_ref, dv_ref,
                  s_ref, kt, vt, qs, dos, dot_ref, ot, dqt, dka, dva):
    _, z, _ = place()
    bf, f32 = jnp.bfloat16, jnp.float32
    fold = SCALE * LOG2E

    def prepare(b, carry):
        rows = pl.ds(mult(b * KB, KB), KB)
        kt[b] = k_ref[rows, :].T
        vt[b] = v_ref[rows, :].T
        dka[b] = jnp.zeros((KB, HEAD), f32)
        dva[b] = jnp.zeros((KB, HEAD), f32)
        return carry

    lax.fori_loop(0, NKB, prepare, 0)
    starts = [jnp.int32(0)]
    for d in range(DOCS - 1):
        starts.append(starts[-1] + len_ref[0, d])

    def tile(t, carry):
        first = (t // 2) * HALF_SEQ + z * CHIP_ROWS + (t % 2) * TOK
        rows = pl.ds(mult(t * TOK, TOK), TOK)
        for h in range(GROUP):
            part = slice(h * HEAD, (h + 1) * HEAD)
            qs[part, :] = q_ref[rows, part]
            grads = do_ref[rows, part]
            dos[part, :] = grads
            dot_ref[:, part] = grads.astype(f32).T
        query_pos = first + lax.broadcasted_iota(jnp.int32, (1, 512), 1) % TOK
        begin = jnp.zeros((1, 512), jnp.int32)
        low = jnp.int32(0)
        for at in starts:
            begin = jnp.where(at <= query_pos, jnp.maximum(begin, at), begin)
            low = jnp.where(at <= first, jnp.maximum(low, at), low)
        kb0 = low // KB
        kb1 = first // KB + 1

        def score(b, top):
            keys = k_ref[pl.ds(mult(b * KB, KB), KB), :]
            s = nt(keys, qs[...])
            key_pos = b * KB + lax.broadcasted_iota(jnp.int32, (KB, 512), 0)
            s = jnp.where((key_pos >= begin) & (key_pos <= query_pos), s, NEG)
            s_ref[b] = s
            return jnp.maximum(top, jnp.max(s, axis=0, keepdims=True))

        top = lax.fori_loop(kb0, kb1, score, jnp.full((1, 512), NEG, f32)) * fold
        ot[...] = jnp.zeros_like(ot)

        def weigh(b, total):
            e = jnp.exp2(s_ref[b] * fold - top)
            s_ref[b] = e
            ot[...] += nn(vt[b], e.astype(bf))
            return total + jnp.sum(e, axis=0, keepdims=True)

        total = lax.fori_loop(kb0, kb1, weigh, jnp.zeros((1, 512), f32))
        inverse = 1.0 / total
        delta = jnp.sum(dot_ref[...] * ot[...], axis=0, keepdims=True) * inverse
        dqt[...] = jnp.zeros_like(dqt)

        def back(b, carry):
            values = v_ref[pl.ds(mult(b * KB, KB), KB), :]
            p = s_ref[b] * inverse
            gp = nt(values, dos[...])
            ds = (p * (gp - delta)).astype(bf)
            dva[b] += nn(p.astype(bf), dos[...])
            dka[b] += nn(ds, qs[...])
            dqt[...] += nn(kt[b], ds)
            return carry

        lax.fori_loop(kb0, kb1, back, 0)
        for h in range(GROUP):
            part = slice(h * HEAD, (h + 1) * HEAD)
            dq_ref[rows, part] = (dqt[:, part] * SCALE).T.astype(bf)
        return carry

    lax.fori_loop(0, GROUP, tile, 0)

    def finish(b, carry):
        rows = pl.ds(mult(b * KB, KB), KB)
        dk_ref[rows, :] = (dka[b] * SCALE).astype(bf)
        dv_ref[rows, :] = dva[b].astype(bf)
        return carry

    lax.fori_loop(0, NKB, finish, 0)


def attend_call(lengths, q, do, k, v):
    bf, f32 = jnp.bfloat16, jnp.float32
    return pl.pallas_call(
        attend_kernel,
        out_shape=(
            jax.ShapeDtypeStruct((512, 512), bf),
            jax.ShapeDtypeStruct((SEQ, HEAD), bf), jax.ShapeDtypeStruct((SEQ, HEAD), bf),
        ),
        in_specs=[SMEM, VMEM, VMEM, VMEM, VMEM],
        out_specs=(VMEM, VMEM, VMEM),
        scratch_shapes=[
            pltpu.VMEM((NKB, KB, 512), f32),
            pltpu.VMEM((NKB, HEAD, KB), bf), pltpu.VMEM((NKB, HEAD, KB), bf),
            pltpu.VMEM((512, HEAD), bf), pltpu.VMEM((512, HEAD), bf),
            pltpu.VMEM((HEAD, 512), f32), pltpu.VMEM((HEAD, 512), f32), pltpu.VMEM((HEAD, 512), f32),
            pltpu.VMEM((NKB, KB, HEAD), f32), pltpu.VMEM((NKB, KB, HEAD), f32),
        ],
        compiler_params=pltpu.CompilerParams(vmem_limit_bytes=48 << 20),
        name="attend",
    )(lengths, q, do, k, v)


def reduce_kernel(dq_ref, dk_ref, dv_ref, hid_ref, qa_ref, qb_ref, va_ref, vb_ref,
                  dql_out, dkl_out, dvl_out, part_out,
                  rb, fin, dql, dkl, dvl, gs, gr, xs, xr, rs, rr, ls):
    bf, f32 = jnp.bfloat16, jnp.float32
    a, z, c = place()
    ids = ring_and_group(a, z, c)
    own = 2 * a + c
    peers = group_peers(a, c)
    ways = (1, -1)
    chunks = ((dk_ref, 1 - a), (dv_ref, 1 - a), (dk_ref, a), (dv_ref, a))
    head_cols = pl.ds(mult(own * HEAD, HEAD), HEAD)
    wide_cols = pl.ds(mult(own * 512, 512), 512)
    mine = pltpu.make_async_copy(
        dq_ref.at[pl.ds(mult(own * TOK, TOK), TOK)], dql.at[:, wide_cols], ls.at[0])
    mine.start()
    enter(ids)
    sent = []

    def rows_of(j, dist):
        y = chunks[j][1]
        return pl.ds(mult(y * HALF_SEQ + ((z + 2 * RING + dist) % RING) * CHIP_ROWS, CHIP_ROWS), CHIP_ROWS)

    def at(w, d, j):
        return (w * 4 + d - 1) * 4 + j

    def starts_far(w, j):
        return (j < 2) == (w == 0)

    def send_on(w, d, j, src):
        cp = remote(src, rb.at[at(w, d, j)], rs.at[at(w, d, j)], rr.at[at(w, d, j)], ids[3 + w])
        cp.start()
        sent.append(cp)

    def arrived(w, d, j):
        slot = rb.at[at(w, d, j)]
        remote(slot, slot, rs.at[at(w, d, j)], rr.at[at(w, d, j)], ids[3 + w]).wait_recv()

    for j in range(4):
        for w in (0, 1):
            if starts_far(w, j):
                send_on(w, 4, j, chunks[j][0].at[rows_of(j, 4)])
    for j in range(4):
        for w in (0, 1):
            if not starts_far(w, j):
                send_on(w, 3, j, chunks[j][0].at[rows_of(j, 3 * ways[w])])
    for p, (pa, pc) in enumerate(peers):
        cp = remote(dq_ref.at[pl.ds(mult((2 * pa + pc) * TOK, TOK), TOK)], dql.at[:, wide_cols],
                    xs.at[p], xr.at[p], ids[p])
        cp.start()
        sent.append(cp)
    hidden = hid_ref[...]
    query_proj = nt(qa_ref[...], hidden).astype(bf)
    value_proj = nt(va_ref[...], hidden).astype(bf)

    def forward(d):
        for j in range(4):
            for w in (0, 1):
                if d == 3 and not starts_far(w, j):
                    continue
                arrived(w, d + 1, j)
                slot = at(w, d + 1, j)
                own_part = chunks[j][0][rows_of(j, d * ways[w]), :].astype(f32)
                rb[slot] = (rb[slot].astype(f32) + own_part).astype(bf)
                send_on(w, d, j, rb.at[slot])

    forward(3)
    forward(2)
    mine.wait()
    for p, (pa, pc) in enumerate(peers):
        cols = pl.ds(mult((2 * pa + pc) * 512, 512), 512)
        remote(dql.at[:, cols], dql.at[:, cols], xs.at[p], xr.at[p], ids[p]).wait_recv()
    query = dql[...]
    dql_out[...] = query
    part_out[:, 4096:6144] = (2.0 * nn(query_proj, query)).astype(bf)
    query_low = nt(qb_ref[...], query).astype(bf)
    part_out[:, 0:4096] = (2.0 * nn(query_low, hidden)).astype(bf)
    forward(1)
    for j in range(4):
        for w in (0, 1):
            arrived(w, 1, j)
        both = rb[at(0, 1, j)].astype(f32) + rb[at(1, 1, j)].astype(f32)
        fin[j] = (both + chunks[j][0][rows_of(j, 0), :].astype(f32)).astype(bf)
        if j == 1:
            for i, dst in enumerate((dkl, dvl)):
                for p in (1, 2):
                    cp = remote(fin.at[i, pl.ds(mult(peers[p][1] * TOK, TOK), TOK)], dst.at[:, head_cols],
                                gs.at[2 * p + i], gr.at[2 * p + i], ids[p])
                    cp.start()
                    sent.append(cp)
    keep = []
    for i, dst in enumerate((dkl, dvl)):
        cp = remote(fin.at[2 + i, pl.ds(mult((1 - c) * TOK, TOK), TOK)], dst.at[:, head_cols],
                    gs.at[i], gr.at[i], ids[0])
        cp.start()
        sent.append(cp)
        one = pltpu.make_async_copy(
            fin.at[2 + i, pl.ds(mult(c * TOK, TOK), TOK)], dst.at[:, head_cols], ls.at[1 + i])
        one.start()
        keep.append(one)
    for one in keep:
        one.wait()
    for p, (pa, pc) in enumerate(peers):
        cols = pl.ds(mult((2 * pa + pc) * HEAD, HEAD), HEAD)
        for i, dst in enumerate((dkl, dvl)):
            remote(dst.at[:, cols], dst.at[:, cols], gs.at[2 * p + i], gr.at[2 * p + i], ids[p]).wait_recv()
    dkl_out[...] = dkl[...]
    value = dvl[...]
    dvl_out[...] = value
    part_out[:, 10240:10752] = (2.0 * nn(value_proj, value)).astype(bf)
    value_low = nt(vb_ref[...], value).astype(bf)
    part_out[:, 6144:10240] = (2.0 * nn(value_low, hidden)).astype(bf)
    part_out[:, 10752:PACKED] = jnp.zeros((RANK, PACKED - 10752), bf)
    for one in sent:
        one.wait_send()


def reduce_call(dq, dk, dv, hidden, qa, qb, va, vb):
    bf = jnp.bfloat16
    dma = pltpu.SemaphoreType.DMA
    return pl.pallas_call(
        reduce_kernel,
        out_shape=(
            jax.ShapeDtypeStruct((TOK, 2048), bf), jax.ShapeDtypeStruct((TOK, 512), bf),
            jax.ShapeDtypeStruct((TOK, 512), bf), jax.ShapeDtypeStruct((RANK, PACKED), bf),
        ),
        in_specs=[VMEM] * 8,
        out_specs=(VMEM,) * 4,
        scratch_shapes=[
            pltpu.VMEM((32, CHIP_ROWS, HEAD), bf), pltpu.VMEM((4, CHIP_ROWS, HEAD), bf),
            pltpu.VMEM((TOK, 2048), bf), pltpu.VMEM((TOK, 512), bf), pltpu.VMEM((TOK, 512), bf),
            dma((6,)), dma((6,)), dma((3,)), dma((3,)), dma((32,)), dma((32,)), dma((3,)),
        ],
        compiler_params=pltpu.CompilerParams(
            collective_id=1, has_side_effects=True, vmem_limit_bytes=40 << 20),
        name="reduce",
    )(dq, dk, dv, hidden, qa, qb, va, vb)


SPANS = ((0, 4096), (4096, 6144), (6144, 10240), (10240, 10752))


def total_kernel(part_ref, qa_out, qb_out, va_out, vb_out,
                 in1, h1, in2, h2, in3, full, s1, r1, s2, r2, s3, r3, s4, r4, s5, r5, ls):
    bf, f32 = jnp.bfloat16, jnp.float32
    a, z, c = place()
    seat = lax.axis_index("dp") * 2 + a
    sibling = {"ctx": ctx_of(a, z, 1 - c)}
    z_of = [(z + d) % RING for d in range(RING)]
    z_ids = [{"ctx": ctx_of(a, zz, c)} for zz in z_of]
    seats = [(seat + e) % 16 for e in range(16)]
    seat_ids = [{"dp": m // 2, "ctx": ctx_of(m % 2, z, c)} for m in seats]
    enter([sibling] + z_ids[1:] + seat_ids[1:])
    sent = []

    def half(which):
        return pl.ds(mult(which * CORE_COLS, CORE_COLS), CORE_COLS)

    one = remote(part_ref.at[:, half(1 - c)], in1, s1, r1, sibling)
    one.start()
    one.wait()
    h1[...] = (part_ref[:, half(c)].astype(f32) + in1[...].astype(f32)).astype(bf)

    def shard(zz):
        return pl.ds(mult(zz * Z_COLS, Z_COLS), Z_COLS)

    copies = []
    for d in range(1, RING):
        one = remote(h1.at[:, shard(z_of[d])], in2.at[d - 1], s2.at[d - 1], r2.at[d - 1], z_ids[d])
        one.start()
        copies.append(one)
    subtotal = h1[:, shard(z)].astype(f32)
    for d in range(1, RING):
        copies[d - 1].wait_recv()
        subtotal = subtotal + in2[d - 1].astype(f32)
    h2[...] = subtotal.astype(bf)
    sent += copies
    copies = []
    for e in range(1, 16):
        one = remote(h2, in3.at[seat], s3.at[e - 1], r3.at[e - 1], seat_ids[e])
        one.start()
        copies.append(one)
    in3[seat] = subtotal.astype(bf)
    for e in range(1, 16):
        slot = in3.at[(seat + 16 - e) % 16]
        remote(slot, slot, s3.at[e - 1], r3.at[e - 1], seat_ids[e]).wait_recv()
    subtotal = in3[0].astype(f32)
    for m in range(1, 16):
        subtotal = subtotal + in3[m].astype(f32)
    sent += copies
    full[c, z] = subtotal.astype(bf)
    copies = []
    for d in range(1, RING):
        one = remote(full.at[c, z], full.at[c, z], s4.at[d - 1], r4.at[d - 1], z_ids[d])
        one.start()
        copies.append(one)
    for d in range(1, RING):
        slot = full.at[c, (z + RING - d) % RING]
        remote(slot, slot, s4.at[d - 1], r4.at[d - 1], z_ids[d]).wait_recv()
    sent += copies
    one = remote(full.at[c], full.at[c], s5, r5, sibling)
    one.start()
    remote(full.at[1 - c], full.at[1 - c], s5, r5, sibling).wait_recv()
    sent.append(one)
    for out, (begin, end) in zip((qa_out, qb_out, va_out, vb_out), SPANS):
        for cc in range(2):
            for zz in range(RING):
                lo = cc * CORE_COLS + zz * Z_COLS
                x, y = max(lo, begin), min(lo + Z_COLS, end)
                if x < y:
                    out[:, x - begin:y - begin] = full[cc, zz, :, x - lo:y - lo].astype(f32)
    for one in sent:
        one.wait_send()


def total_call(part):
    bf, f32 = jnp.bfloat16, jnp.float32
    dma = pltpu.SemaphoreType.DMA
    return pl.pallas_call(
        total_kernel,
        out_shape=tuple(jax.ShapeDtypeStruct((RANK, e - b), f32) for b, e in SPANS),
        in_specs=[VMEM],
        out_specs=(VMEM,) * 4,
        scratch_shapes=[
            pltpu.VMEM((RANK, CORE_COLS), bf), pltpu.VMEM((RANK, CORE_COLS), bf),
            pltpu.VMEM((RING - 1, RANK, Z_COLS), bf), pltpu.VMEM((RANK, Z_COLS), bf),
            pltpu.VMEM((16, RANK, Z_COLS), bf), pltpu.VMEM((2, RING, RANK, Z_COLS), bf),
            dma, dma, dma((7,)), dma((7,)), dma((15,)), dma((15,)), dma((7,)), dma((7,)), dma, dma,
            dma,
        ],
        compiler_params=pltpu.CompilerParams(collective_id=2, has_side_effects=True),
        name="total",
    )(part)


def shards(q, k, v, do, hidden, lengths, qa, qb, va, vb):
    qg, dog, kg, vg = gather_call(q[0], do[0], k[0], v[0])
    dq, dk, dv = attend_call(lengths, qg, dog, kg, vg)
    dql, dkl, dvl, part = reduce_call(dq, dk, dv, hidden[0], qa, qb, va, vb)
    sums = total_call(part)
    return (dql[None], dkl[None], dvl[None]) + tuple(sums)


def solution(mesh):
    token = P("dp", "ctx", None)
    return jax.shard_map(
        shards,
        mesh=mesh,
        in_specs=(token, token, token, token, token, P("dp", None), P(), P(), P(), P()),
        out_specs=(token, token, token, P(), P(), P(), P()),
        check_vma=False,
    )
```

time: 835 us -> 145 us (0.17)
  waiting for transfers between devices: 696 us -> 0 us
  Pallas kernels: 0 us -> 132 us
  local copies, waits for them, and re-layouts: 62 us -> 11.4 us
  other arithmetic: 28 us -> 0 us
  matrix products: 19.9 us -> 0 us
  between operations: 14 us -> 0.75 us
  loops' own time: 11.5 us -> 0 us
    reduce_scatter x1 -> x0, waiting for transfers between devices: 336 us -> none  [sent_together(): lax.psum_scatter(both, axis, scatter_dimension=dim, tiled=True)]
    psum x1 -> x0, waiting for transfers between devices: 257 us -> none  [packed_total(): subtotal = lax.psum(jnp.concatenate([a.ravel() for a in arrays]), axis)]
    pallas_call x0 -> x4, Pallas kernels: none -> 132 us  [the longest x1 39.3 us: reduce_call(): pl.pallas_call(reduce_kernel, out_shape=(jax.ShapeDtypeStruct((TOK, 2048)...]
    all_gather x1 -> x0, waiting for transfers between devices: 104 us -> none  [in_one_piece(): lax.all_gather(both, axis, axis=dim, tiled=True)]
    dot_general x11 -> x0, matrix products: 19.9 us -> none  [the longest x4 4.14 us: contract_first(): lax.dot_general(left, right, (((0,), (0,)), ((), ())), preferred_element_...]
    while x4 -> x0, local copies, waits for them, and re-layouts: 17.5 us -> none  [walk_keys(): return lax.fori_loop(0, piece_rows // rows_per_block, one_block, carry_in)]
    another operation x6 -> x0, local copies, waits for them, and re-layouts: 13.3 us -> none
    another operation x18 -> x0, loops' own time: 11.5 us -> none  [the longest x2 11.1 us: walk_keys(): return lax.fori_loop(0, piece_rows // rows_per_block, one_block, carry_in)]
  transfers between devices with their start and end apart: 3 -> 0, of which waited for: 3 -> 0; matrix products, arithmetic and copies ran while one was open for 2% -> 0% of each run, Pallas kernels for 0% -> 0%
where the time goes in v1:
time: 145 us; the launch traced here: 144 us
  Pallas kernels  132 us (91%)
  local copies, waits for them, and re-layouts  11.4 us (8%)
    pallas_call x1, Pallas kernels, reduce_call(): pl.pallas_call(reduce_kernel, out_shape=(jax.ShapeDtypeStruct((TOK, 2048)...  39.3 us
    pallas_call x1, Pallas kernels, total_call(): pl.pallas_call(total_kernel, out_shape=tuple((jax.ShapeDtypeStruct((RANK,...  36.8 us
    pallas_call x1, Pallas kernels, gather_call(): pl.pallas_call(gather_kernel, out_shape=(jax.ShapeDtypeStruct((512, 512),...  36.3 us
    pallas_call x1, Pallas kernels, attend_call(): pl.pallas_call(attend_kernel, out_shape=(jax.ShapeDtypeStruct((512, 512),...  19.8 us
    unnamed x37, local copies, waits for them, and re-layouts  11.4 us

profile of v1, /device:TPU:1, one launch (start us, length us, event | category | flops | bytes accessed | tf_op | source)
XLA Modules:
  0.0 144.4 jit_solution(10056965244872851435)
XLA Ops:
  0.6 36.3 %gather.1 = (bf16[512,512]{1,0:T(8,128)(2,1)}, bf16[512,512]{1,0:T(8,128)(2,1)}, bf16[4096,128]{1,0:T(8,128)(2,1)}, bf16[4096,128]{1,0:T(8,128)(2,1)}) custom-call(bf16[128,2048]{1,0:T(8,128)(2,1)} %bitcast.12, bf16[128,2048]{1,0:T(8,128)(2,1)} %bitcast.13, bf16[128,512]{1,0:T(8,128)(2,1)} %bitcast.14, bf16[128,512]{1,0:T(8,128)(2,1)} %bitcast.15), custom_call_target="tpu_custom_call" | custom-call | tf_op jit(solution)/shard_map/gather/pallas_call | solution.py:182
  36.9 0.0 copy-start.10
  36.9 0.6 copy-done.10
  37.6 0.0 copy-start
  37.6 1.2 copy-done
  38.8 0.0 copy-start.1
  38.8 1.2 copy-done.1
  40.0 0.0 copy-start.3
  40.0 1.0 copy-done.3
  41.1 0.0 copy-start.4
  41.1 1.0 copy-done.4
  42.1 0.0 copy-start.2
  42.1 0.0 copy-start.6
  42.1 0.0 copy-start.7
  42.1 0.0 copy-start.8
  42.1 0.0 copy-start.9
  42.1 19.8 %attend.1 = (bf16[512,512]{1,0:T(8,128)(2,1)S(1)}, bf16[4096,128]{1,0:T(8,128)(2,1)S(1)}, bf16[4096,128]{1,0:T(8,128)(2,1)S(1)}) custom-call(s32[1,16]{1,0:T(1,128)S(1)} %copy-done.10, bf16[512,512]{1,0:T(8,128)(2,1)S(1)} %copy-done.3, bf16[512,512]{1,0:T(8,128)(2,1)S(1)} %copy-done.4, bf16[4096,128]{1,0:T(8,128)(2,1)S(1)} %copy-done, ...), custom_call_target="tpu_custom_call" | custom-call | tf_op jit(solution)/shard_map/attend/pallas_call | solution.py:288
  61.9 0.0 copy-done.2
  61.9 0.0 copy-done.6
  62.0 0.0 copy-done.7
  62.0 0.0 copy-done.8
  62.0 0.0 copy-done.9
  62.0 39.3 %reduce.1 = (bf16[128,2048]{1,0:T(8,128)(2,1)S(1)}, bf16[128,512]{1,0:T(8,128)(2,1)S(1)}, bf16[128,512]{1,0:T(8,128)(2,1)S(1)}, bf16[16,12288]{1,0:T(8,128)(2,1)S(1)}) custom-call(bf16[512,512]{1,0:T(8,128)(2,1)S(1)} %get-tuple-element.26.dq_ref, bf16[4096,128]{1,0:T(8,128)(2,1)S(1)} %get-tuple-element.27.dk_ref, ...), custom_call_target="tpu_custom_call" | custom-call | tf_op jit(solution)/shard_map/reduce/pallas_call | solution.py:427
  101.3 0.0 copy-start.5
  101.3 0.7 copy-done.5
  102.0 36.8 %total.1 = (f32[16,4096]{1,0:T(8,128)}, f32[16,2048]{1,0:T(8,128)}, f32[16,4096]{1,0:T(8,128)}, f32[16,512]{1,0:T(8,128)}) custom-call(bf16[16,12288]{1,0:T(8,128)(2,1)} %copy-done.5), custom_call_target="tpu_custom_call" | custom-call | tf_op jit(solution)/shard_map/total/pallas_call | solution.py:525
  138.9 0.8 copy.24
  139.7 0.0 copy-start.12
  139.7 0.7 copy.25
  140.3 0.7 copy.26
  141.0 0.0 copy-done.12
  141.0 0.0 copy-start.13
  141.0 0.7 copy.27
  141.7 0.3 copy-done.13
  142.0 0.0 copy-start.11
  142.0 0.7 copy.28
  142.6 0.3 copy-done.11
  143.0 0.0 copy-start.14
  143.0 0.7 copy.29
  143.7 0.1 copy-done.14
  143.7 0.6 copy.30
Async XLA Ops:
  36.9 0.7 copy-start.10
  37.6 1.2 copy-start
  38.8 1.2 copy-start.1
  40.0 1.0 copy-start.3
  41.1 1.0 copy-start.4
  42.1 19.8 %copy-start.2 = (bf16[1,128,4096]{2,1,0:T(8,128)(2,1)S(1)}, bf16[1,128,4096]{2,1,0:T(8,128)(2,1)}, u32[]{:S(2)}) copy-start(bf16[1,128,4096]{2,1,0:T(8,128)(2,1)} %param.14) | copy-start | bytes 3145732
  42.1 19.8 %copy-start.6 = (bf16[16,4096]{1,0:T(8,128)(2,1)S(1)}, bf16[16,4096]{1,0:T(8,128)(2,1)}, u32[]{:S(2)}) copy-start(bf16[16,4096]{1,0:T(8,128)(2,1)} %qa_ref.1) | copy-start | bytes 393220
  42.1 19.9 %copy-start.7 = (bf16[16,4096]{1,0:T(8,128)(2,1)S(1)}, bf16[16,4096]{1,0:T(8,128)(2,1)}, u32[]{:S(2)}) copy-start(bf16[16,4096]{1,0:T(8,128)(2,1)} %va_ref.1) | copy-start | bytes 393220
  42.1 19.9 %copy-start.8 = (bf16[16,2048]{1,0:T(8,128)(2,1)S(1)}, bf16[16,2048]{1,0:T(8,128)(2,1)}, u32[]{:S(2)}) copy-start(bf16[16,2048]{1,0:T(8,128)(2,1)} %qb_ref.1) | copy-start | bytes 196612
  42.1 19.9 %copy-start.9 = (bf16[16,512]{1,0:T(8,128)(2,1)S(1)}, bf16[16,512]{1,0:T(8,128)(2,1)}, u32[]{:S(2)}) copy-start(bf16[16,512]{1,0:T(8,128)(2,1)} %vb_ref.1) | copy-start | bytes 49156
  101.3 0.7 copy-start.5
  139.7 1.3 copy-start.12
  141.0 1.0 copy-start.13
  142.0 1.0 copy-start.11
  143.0 0.8 copy-start.14

commit v2 on v1

v2 whole, which is shorter than its diff:
```python
import math

import jax
import jax.numpy as jnp
from jax import lax
from jax.experimental import pallas as pl
from jax.experimental.pallas import tpu as pltpu
from jax.sharding import PartitionSpec as P

MESH = pl.DeviceIdType.MESH
HEAD = 128
GROUP = 4
TOK = 128
RING = 8
CHIP_ROWS = 256
HALF_SEQ = 2048
SEQ = 4096
KB = 256
WIDE = GROUP * CHIP_ROWS
NKB = SEQ // KB
RANK = 16
PACKED = 6144
CORE_COLS = PACKED // 2
Z_COLS = CORE_COLS // RING
DOCS = 16
NEG = -1e30
SCALE = HEAD ** (-0.5)
LOG2E = math.log2(math.e)
ANY = pl.BlockSpec(memory_space=pl.ANY)
VMEM = pl.BlockSpec(memory_space=pltpu.VMEM)
SMEM = pl.BlockSpec(memory_space=pltpu.SMEM)


def nn(left, right):
    return lax.dot_general(left, right, (((1,), (0,)), ((), ())), preferred_element_type=jnp.float32)


def nt(left, right):
    return lax.dot_general(left, right, (((1,), (1,)), ((), ())), preferred_element_type=jnp.float32)


def place():
    me = lax.axis_index("ctx")
    return me // 16, (me // 2) % RING, me % 2


def ctx_of(a, z, c):
    return a * 16 + z * 2 + c


def mult(value, of):
    return pl.multiple_of(value, of)


def group_peers(a, c):
    return ((a, 1 - c), (1 - a, c), (1 - a, 1 - c))


def enter(ids):
    barrier = pltpu.get_barrier_semaphore()
    for one in ids:
        pl.semaphore_signal(barrier, inc=1, device_id=one, device_id_type=MESH)
    pl.semaphore_wait(barrier, len(ids))


def remote(src, dst, ssem, rsem, to):
    return pltpu.make_async_remote_copy(
        src_ref=src, dst_ref=dst, send_sem=ssem, recv_sem=rsem, device_id=to, device_id_type=MESH
    )


def ring_and_group(a, z, c):
    ids = [{"ctx": ctx_of(pa, z, pc)} for pa, pc in group_peers(a, c)]
    ids.append({"ctx": ctx_of(a, (z + 1) % RING, c)})
    ids.append({"ctx": ctx_of(a, (z + RING - 1) % RING, c)})
    return ids


def gather_kernel(q_ref, do_ref, k_ref, v_ref, qg_ref, dog_ref, kg_ref, vg_ref,
                  kall, vall, qall, doall, gs, gr, xs, xr, rs, rr, ls):
    a, z, c = place()
    ids = ring_and_group(a, z, c)
    own = 2 * a + c
    row0 = mult(a * HALF_SEQ + z * CHIP_ROWS + c * TOK, TOK)
    local = []
    for i, (src, dst) in enumerate(((k_ref, kall), (v_ref, vall))):
        local.append(pltpu.make_async_copy(
            src.at[:, pl.ds(mult(own * HEAD, HEAD), HEAD)], dst.at[pl.ds(row0, TOK)], ls.at[i]))
    wide = []
    for i, (src, dst) in enumerate(((q_ref, qall), (do_ref, doall))):
        wide.append(pltpu.make_async_copy(
            src.at[:, pl.ds(mult(own * 512, 512), 512)],
            dst.at[pl.ds(mult(own * TOK, TOK), TOK)], ls.at[2 + i]))
    for one in local + wide:
        one.start()
    enter(ids)
    sent = []
    peers = group_peers(a, c)
    for p, (pa, pc) in enumerate(peers):
        for i, (src, dst) in enumerate(((k_ref, kall), (v_ref, vall))):
            head = 2 * pa + pc
            cp = remote(src.at[:, pl.ds(mult(head * HEAD, HEAD), HEAD)], dst.at[pl.ds(row0, TOK)],
                        gs.at[2 * p + i], gr.at[2 * p + i], ids[p])
            cp.start()
            sent.append(cp)
    for p, (pa, pc) in enumerate(peers):
        for i, (src, dst) in enumerate(((q_ref, qall), (do_ref, doall))):
            head = 2 * pa + pc
            cp = remote(src.at[:, pl.ds(mult(head * 512, 512), 512)],
                        dst.at[pl.ds(mult(own * TOK, TOK), TOK)],
                        xs.at[2 * p + i], xr.at[2 * p + i], ids[p])
            cp.start()
            sent.append(cp)

    def group_arrived(p):
        pa, pc = peers[p]
        rows = pl.ds(mult(pa * HALF_SEQ + z * CHIP_ROWS + pc * TOK, TOK), TOK)
        for i, dst in enumerate((kall, vall)):
            remote(dst.at[rows], dst.at[rows], gs.at[2 * p + i], gr.at[2 * p + i], ids[p]).wait_recv()

    chunks = ((kall, a), (vall, a), (kall, 1 - a), (vall, 1 - a))
    ways = (1, -1)

    def chunk(j, zz):
        ref, y = chunks[j]
        return ref.at[pl.ds(mult(y * HALF_SEQ + zz * CHIP_ROWS, CHIP_ROWS), CHIP_ROWS)]

    def at(w, s, j):
        return (w * 4 + s) * 4 + j

    def send_on(w, s, j):
        part = chunk(j, (z + 2 * RING - ways[w] * s) % RING)
        cp = remote(part, part, rs.at[at(w, s, j)], rr.at[at(w, s, j)], ids[3 + w])
        cp.start()
        sent.append(cp)

    def arrived(w, s, j):
        part = chunk(j, (z + 2 * RING - ways[w] * (s + 1)) % RING)
        remote(part, part, rs.at[at(w, s, j)], rr.at[at(w, s, j)], ids[3 + w]).wait_recv()

    def carries(w, s, j):
        return s < 3 or (j < 2) == (w == 0)

    for one in local:
        one.wait()
    group_arrived(0)
    for j in (0, 1):
        for w in (0, 1):
            send_on(w, 0, j)
    group_arrived(1)
    group_arrived(2)
    for j in (2, 3):
        for w in (0, 1):
            send_on(w, 0, j)
    for s in range(4):
        for j in range(4):
            for w in (0, 1):
                if carries(w, s, j):
                    arrived(w, s, j)
                    if s < 3 and carries(w, s + 1, j):
                        send_on(w, s + 1, j)
    kg_ref[...] = kall[...]
    vg_ref[...] = vall[...]
    for one in wide:
        one.wait()
    for p, (pa, pc) in enumerate(peers):
        rows = pl.ds(mult((2 * pa + pc) * TOK, TOK), TOK)
        for i, dst in enumerate((qall, doall)):
            remote(dst.at[rows], dst.at[rows], xs.at[2 * p + i], xr.at[2 * p + i], ids[p]).wait_recv()
    qg_ref[...] = qall[...]
    dog_ref[...] = doall[...]
    for one in sent:
        one.wait_send()


def gather_call(q, do, k, v):
    bf = jnp.bfloat16
    dma = pltpu.SemaphoreType.DMA
    return pl.pallas_call(
        gather_kernel,
        out_shape=(
            jax.ShapeDtypeStruct((512, 512), bf), jax.ShapeDtypeStruct((512, 512), bf),
            jax.ShapeDtypeStruct((SEQ, HEAD), bf), jax.ShapeDtypeStruct((SEQ, HEAD), bf),
        ),
        in_specs=[ANY, ANY, VMEM, VMEM],
        out_specs=(VMEM,) * 4,
        scratch_shapes=[
            pltpu.VMEM((SEQ, HEAD), bf), pltpu.VMEM((SEQ, HEAD), bf),
            pltpu.VMEM((512, 512), bf), pltpu.VMEM((512, 512), bf),
            dma((6,)), dma((6,)), dma((6,)), dma((6,)), dma((32,)), dma((32,)), dma((4,)),
        ],
        compiler_params=pltpu.CompilerParams(
            collective_id=0, has_side_effects=True, vmem_limit_bytes=14 << 20),
        name="gather",
    )(q, do, k, v)


def attend_kernel(len_ref, q_ref, do_ref, k_ref, v_ref, dq_ref, dk_ref, dv_ref,
                  s_ref, kt, vt, qs, dos, dot_ref, ot, dqt, dka, dva):
    _, z, _ = place()
    bf, f32 = jnp.bfloat16, jnp.float32
    fold = SCALE * LOG2E

    def prepare(b, carry):
        rows = pl.ds(mult(b * KB, KB), KB)
        kt[b] = k_ref[rows, :].T
        vt[b] = v_ref[rows, :].T
        dka[b] = jnp.zeros((KB, HEAD), f32)
        dva[b] = jnp.zeros((KB, HEAD), f32)
        return carry

    lax.fori_loop(0, NKB, prepare, 0)
    starts = [jnp.int32(0)]
    for d in range(DOCS - 1):
        starts.append(starts[-1] + len_ref[0, d])

    def tile(t, carry):
        first = t * HALF_SEQ + z * CHIP_ROWS
        rows = pl.ds(mult(t * CHIP_ROWS, CHIP_ROWS), CHIP_ROWS)
        for h in range(GROUP):
            part = slice(h * HEAD, (h + 1) * HEAD)
            stack = slice(h * CHIP_ROWS, (h + 1) * CHIP_ROWS)
            qs[stack, :] = q_ref[rows, part]
            grads = do_ref[rows, part]
            dos[stack, :] = grads
            dot_ref[:, stack] = grads.astype(f32).T
        query_pos = first + lax.broadcasted_iota(jnp.int32, (1, WIDE), 1) % CHIP_ROWS
        begin = jnp.zeros((1, WIDE), jnp.int32)
        low, high = jnp.int32(0), jnp.int32(0)
        for at in starts:
            begin = jnp.where(at <= query_pos, jnp.maximum(begin, at), begin)
            low = jnp.where(at <= first, jnp.maximum(low, at), low)
            high = jnp.where(at < first + CHIP_ROWS, jnp.maximum(high, at), high)
        kb0 = low // KB
        kb1 = first // KB + 1
        kbm = jnp.minimum((high + KB - 1) // KB, kb1 - 1)

        def score(b, top):
            keys = k_ref[pl.ds(mult(b * KB, KB), KB), :]
            s = nt(keys, qs[...])
            s_ref[b] = s
            return jnp.maximum(top, jnp.max(s, axis=0, keepdims=True))

        def score_masked(b, top):
            keys = k_ref[pl.ds(mult(b * KB, KB), KB), :]
            s = nt(keys, qs[...])
            key_pos = b * KB + lax.broadcasted_iota(jnp.int32, (KB, WIDE), 0)
            s = jnp.where((key_pos >= begin) & (key_pos <= query_pos), s, NEG)
            s_ref[b] = s
            return jnp.maximum(top, jnp.max(s, axis=0, keepdims=True))

        top = score_masked(kb1 - 1, jnp.full((1, WIDE), NEG, f32))
        top = lax.fori_loop(kb0, kbm, score_masked, top)
        top = lax.fori_loop(kbm, kb1 - 1, score, top) * fold
        ot[...] = jnp.zeros_like(ot)

        def weigh(b, total):
            e = jnp.exp2(s_ref[b] * fold - top)
            s_ref[b] = e
            ot[...] += nn(vt[b], e.astype(bf))
            return total + jnp.sum(e, axis=0, keepdims=True)

        total = lax.fori_loop(kb0, kb1, weigh, jnp.zeros((1, WIDE), f32))
        inverse = 1.0 / total
        delta = jnp.sum(dot_ref[...] * ot[...], axis=0, keepdims=True) * inverse
        dqt[...] = jnp.zeros_like(dqt)

        def back(b, carry):
            values = v_ref[pl.ds(mult(b * KB, KB), KB), :]
            p = s_ref[b] * inverse
            gp = nt(values, dos[...])
            ds = (p * (gp - delta)).astype(bf)
            dva[b] += nn(p.astype(bf), dos[...])
            dka[b] += nn(ds, qs[...])
            dqt[...] += nn(kt[b], ds)
            return carry

        lax.fori_loop(kb0, kb1, back, 0)
        for h in range(GROUP):
            part = slice(h * HEAD, (h + 1) * HEAD)
            stack = slice(h * CHIP_ROWS, (h + 1) * CHIP_ROWS)
            dq_ref[rows, part] = (dqt[:, stack] * SCALE).T.astype(bf)
        return carry

    lax.fori_loop(0, 2, tile, 0)

    def finish(b, carry):
        rows = pl.ds(mult(b * KB, KB), KB)
        dk_ref[rows, :] = (dka[b] * SCALE).astype(bf)
        dv_ref[rows, :] = dva[b].astype(bf)
        return carry

    lax.fori_loop(0, NKB, finish, 0)


def attend_call(lengths, q, do, k, v):
    bf, f32 = jnp.bfloat16, jnp.float32
    return pl.pallas_call(
        attend_kernel,
        out_shape=(
            jax.ShapeDtypeStruct((512, 512), bf),
            jax.ShapeDtypeStruct((SEQ, HEAD), bf), jax.ShapeDtypeStruct((SEQ, HEAD), bf),
        ),
        in_specs=[SMEM, VMEM, VMEM, VMEM, VMEM],
        out_specs=(VMEM, VMEM, VMEM),
        scratch_shapes=[
            pltpu.VMEM((NKB, KB, WIDE), f32),
            pltpu.VMEM((NKB, HEAD, KB), bf), pltpu.VMEM((NKB, HEAD, KB), bf),
            pltpu.VMEM((WIDE, HEAD), bf), pltpu.VMEM((WIDE, HEAD), bf),
            pltpu.VMEM((HEAD, WIDE), f32), pltpu.VMEM((HEAD, WIDE), f32), pltpu.VMEM((HEAD, WIDE), f32),
            pltpu.VMEM((NKB, KB, HEAD), f32), pltpu.VMEM((NKB, KB, HEAD), f32),
        ],
        compiler_params=pltpu.CompilerParams(vmem_limit_bytes=46 << 20),
        name="attend",
    )(lengths, q, do, k, v)


def reduce_kernel(dq_ref, dk_ref, dv_ref, hid_ref, qa_ref, qb_ref, va_ref, vb_ref,
                  dql_out, dkl_out, dvl_out, full_out,
                  rb, fin, dql, dkl, dvl, part, in1, h1, in2, h2, in3, full,
                  gs, gr, xs, xr, rs, rr, ls,
                  s1, r1, s2, r2, s3, r3, s4, r4, s5, r5):
    bf, f32 = jnp.bfloat16, jnp.float32
    a, z, c = place()
    ids = ring_and_group(a, z, c)
    own = 2 * a + c
    peers = group_peers(a, c)
    ways = (1, -1)
    chunks = ((dk_ref, 1 - a), (dv_ref, 1 - a), (dk_ref, a), (dv_ref, a))
    head_cols = pl.ds(mult(own * HEAD, HEAD), HEAD)
    wide_cols = pl.ds(mult(own * 512, 512), 512)
    seat = lax.axis_index("dp") * 2 + a
    sibling = ids[0]
    z_of = [(z + d) % RING for d in range(RING)]
    z_ids = [{"ctx": ctx_of(a, zz, c)} for zz in z_of]
    seats = [(seat + e) % 16 for e in range(16)]
    seat_ids = [{"dp": m // 2, "ctx": ctx_of(m % 2, z, c)} for m in seats]
    mine = pltpu.make_async_copy(
        dq_ref.at[pl.ds(mult(own * TOK, TOK), TOK)], dql.at[:, wide_cols], ls.at[0])
    mine.start()
    enter([sibling, ids[2]] + z_ids[1:] + seat_ids[1:])
    sent = []

    def go(src, dst, ssem, rsem, to):
        cp = remote(src, dst, ssem, rsem, to)
        cp.start()
        sent.append(cp)

    def came(dst, ssem, rsem, to):
        remote(dst, dst, ssem, rsem, to).wait_recv()

    def rows_of(j, dist):
        y = chunks[j][1]
        return pl.ds(mult(y * HALF_SEQ + ((z + 2 * RING + dist) % RING) * CHIP_ROWS, CHIP_ROWS), CHIP_ROWS)

    def at(w, d, j):
        return (w * 4 + d - 1) * 4 + j

    def starts_far(w, j):
        return (j < 2) == (w == 0)

    def send_on(w, d, j, src):
        k = at(w, d, j)
        go(src, rb.at[k], rs.at[k], rr.at[k], ids[3 + w])

    def arrived(w, d, j):
        k = at(w, d, j)
        came(rb.at[k], rs.at[k], rr.at[k], ids[3 + w])

    def half(which):
        return pl.ds(mult(which * CORE_COLS, CORE_COLS), CORE_COLS)

    def shard(zz):
        return pl.ds(mult(zz * Z_COLS, Z_COLS), Z_COLS)

    def core_send(u):
        go(part.at[u, :, half(1 - c)], in1.at[u], s1.at[u], r1.at[u], sibling)

    def z_send(u):
        came(in1.at[u], s1.at[u], r1.at[u], sibling)
        h1[u] = (part[u, :, half(c)].astype(f32) + in1[u].astype(f32)).astype(bf)
        for d in range(1, RING):
            k = u * 7 + d - 1
            go(h1.at[u, :, shard(z_of[d])], in2.at[k], s2.at[k], r2.at[k], z_ids[d])

    def seat_send(u):
        subtotal = h1[u, :, shard(z)].astype(f32)
        for d in range(1, RING):
            k = u * 7 + d - 1
            came(in2.at[k], s2.at[k], r2.at[k], z_ids[d])
            subtotal = subtotal + in2[k].astype(f32)
        h2[u] = subtotal.astype(bf)
        for e in range(1, 16):
            k = u * 15 + e - 1
            go(h2.at[u], in3.at[u, seat], s3.at[k], r3.at[k], seat_ids[e])
        in3[u, seat] = subtotal.astype(bf)

    def z_spread(u):
        for e in range(1, 16):
            k = u * 15 + e - 1
            came(in3.at[u, (seat + 16 - e) % 16], s3.at[k], r3.at[k], seat_ids[e])
        subtotal = in3[u, 0].astype(f32)
        for m in range(1, 16):
            subtotal = subtotal + in3[u, m].astype(f32)
        full[u, c, z] = subtotal.astype(bf)
        for d in range(1, RING):
            k = u * 7 + d - 1
            go(full.at[u, c, z], full.at[u, c, z], s4.at[k], r4.at[k], z_ids[d])

    def core_spread(u):
        for d in range(1, RING):
            k = u * 7 + d - 1
            came(full.at[u, c, (z + RING - d) % RING], s4.at[k], r4.at[k], z_ids[d])
        go(full.at[u, c], full.at[u, c], s5.at[u], r5.at[u], sibling)

    def collect(u):
        came(full.at[u, 1 - c], s5.at[u], r5.at[u], sibling)
        full_out[u] = full[u]

    for j in range(4):
        for w in (0, 1):
            if starts_far(w, j):
                send_on(w, 4, j, chunks[j][0].at[rows_of(j, 4)])
    for j in range(4):
        for w in (0, 1):
            if not starts_far(w, j):
                send_on(w, 3, j, chunks[j][0].at[rows_of(j, 3 * ways[w])])
    for p, (pa, pc) in enumerate(peers):
        go(dq_ref.at[pl.ds(mult((2 * pa + pc) * TOK, TOK), TOK)], dql.at[:, wide_cols],
           xs.at[p], xr.at[p], ids[p])
    hidden = hid_ref[...]
    query_proj = nt(qa_ref[...], hidden).astype(bf)
    value_proj = nt(va_ref[...], hidden).astype(bf)
    part[1, :, 4608:PACKED] = jnp.zeros((RANK, PACKED - 4608), bf)

    def forward(d):
        for j in range(4):
            for w in (0, 1):
                if d == 3 and not starts_far(w, j):
                    continue
                arrived(w, d + 1, j)
                slot = at(w, d + 1, j)
                own_part = chunks[j][0][rows_of(j, d * ways[w]), :].astype(f32)
                rb[slot] = (rb[slot].astype(f32) + own_part).astype(bf)
                send_on(w, d, j, rb.at[slot])

    forward(3)
    mine.wait()
    for p, (pa, pc) in enumerate(peers):
        cols = pl.ds(mult((2 * pa + pc) * 512, 512), 512)
        came(dql.at[:, cols], xs.at[p], xr.at[p], ids[p])
    query = dql[...]
    dql_out[...] = query
    part[0, :, 4096:6144] = (2.0 * nn(query_proj, query)).astype(bf)
    query_low = nt(qb_ref[...], query).astype(bf)
    part[0, :, 0:4096] = (2.0 * nn(query_low, hidden)).astype(bf)
    core_send(0)
    forward(2)
    z_send(0)
    forward(1)
    seat_send(0)
    for j in range(4):
        for w in (0, 1):
            arrived(w, 1, j)
        both = rb[at(0, 1, j)].astype(f32) + rb[at(1, 1, j)].astype(f32)
        fin[j] = (both + chunks[j][0][rows_of(j, 0), :].astype(f32)).astype(bf)
        if j == 1:
            for i, dst in ((1, dvl), (0, dkl)):
                for p in (1, 2):
                    go(fin.at[i, pl.ds(mult(peers[p][1] * TOK, TOK), TOK)], dst.at[:, head_cols],
                       gs.at[2 * p + i], gr.at[2 * p + i], ids[p])
    keep = []
    for i, dst in ((1, dvl), (0, dkl)):
        go(fin.at[2 + i, pl.ds(mult((1 - c) * TOK, TOK), TOK)], dst.at[:, head_cols],
           gs.at[i], gr.at[i], ids[0])
        one = pltpu.make_async_copy(
            fin.at[2 + i, pl.ds(mult(c * TOK, TOK), TOK)], dst.at[:, head_cols], ls.at[1 + i])
        one.start()
        keep.append(one)
    for one in keep:
        one.wait()

    def returned(i, dst):
        for p, (pa, pc) in enumerate(peers):
            cols = pl.ds(mult((2 * pa + pc) * HEAD, HEAD), HEAD)
            came(dst.at[:, cols], gs.at[2 * p + i], gr.at[2 * p + i], ids[p])

    returned(1, dvl)
    value = dvl[...]
    part[1, :, 4096:4608] = (2.0 * nn(value_proj, value)).astype(bf)
    value_low = nt(vb_ref[...], value).astype(bf)
    part[1, :, 0:4096] = (2.0 * nn(value_low, hidden)).astype(bf)
    core_send(1)
    dvl_out[...] = value
    z_send(1)
    z_spread(0)
    seat_send(1)
    core_spread(0)
    returned(0, dkl)
    dkl_out[...] = dkl[...]
    z_spread(1)
    collect(0)
    core_spread(1)
    collect(1)
    for one in sent:
        one.wait_send()


def reduce_call(dq, dk, dv, hidden, qa, qb, va, vb):
    bf = jnp.bfloat16
    dma = pltpu.SemaphoreType.DMA
    return pl.pallas_call(
        reduce_kernel,
        out_shape=(
            jax.ShapeDtypeStruct((TOK, 2048), bf), jax.ShapeDtypeStruct((TOK, 512), bf),
            jax.ShapeDtypeStruct((TOK, 512), bf),
            jax.ShapeDtypeStruct((2, 2, RING, RANK, Z_COLS), bf),
        ),
        in_specs=[VMEM] * 8,
        out_specs=(VMEM,) * 4,
        scratch_shapes=[
            pltpu.VMEM((32, CHIP_ROWS, HEAD), bf), pltpu.VMEM((4, CHIP_ROWS, HEAD), bf),
            pltpu.VMEM((TOK, 2048), bf), pltpu.VMEM((TOK, 512), bf), pltpu.VMEM((TOK, 512), bf),
            pltpu.VMEM((2, RANK, PACKED), bf), pltpu.VMEM((2, RANK, CORE_COLS), bf),
            pltpu.VMEM((2, RANK, CORE_COLS), bf), pltpu.VMEM((14, RANK, Z_COLS), bf),
            pltpu.VMEM((2, RANK, Z_COLS), bf), pltpu.VMEM((2, 16, RANK, Z_COLS), bf),
            pltpu.VMEM((2, 2, RING, RANK, Z_COLS), bf),
            dma((6,)), dma((6,)), dma((3,)), dma((3,)), dma((32,)), dma((32,)), dma((3,)),
            dma((2,)), dma((2,)), dma((14,)), dma((14,)), dma((30,)), dma((30,)),
            dma((14,)), dma((14,)), dma((2,)), dma((2,)),
        ],
        compiler_params=pltpu.CompilerParams(
            collective_id=1, has_side_effects=True, vmem_limit_bytes=24 << 20),
        name="reduce",
    )(dq, dk, dv, hidden, qa, qb, va, vb)


SPANS = ((0, 0, 4096), (0, 4096, 6144), (1, 0, 4096), (1, 4096, 4608))


def finish_kernel(dql_ref, dkl_ref, dvl_ref, full_ref, dq_out, dk_out, dv_out,
                  qa_out, qb_out, va_out, vb_out, sem):
    copies = []
    for i, (src, dst) in enumerate(((dql_ref, dq_out), (dkl_ref, dk_out), (dvl_ref, dv_out))):
        copies.append(pltpu.make_async_copy(src, dst, sem.at[i]))
    for one in copies:
        one.start()
    for out, (u, begin, end) in zip((qa_out, qb_out, va_out, vb_out), SPANS):
        for cc in range(2):
            for zz in range(RING):
                lo = cc * CORE_COLS + zz * Z_COLS
                x, y = max(lo, begin), min(lo + Z_COLS, end)
                if x < y:
                    out[:, x - begin:y - begin] = full_ref[u, cc, zz, :, x - lo:y - lo].astype(jnp.float32)
    for one in copies:
        one.wait()


def finish_call(dql, dkl, dvl, full):
    bf = jnp.bfloat16
    return pl.pallas_call(
        finish_kernel,
        out_shape=(
            jax.ShapeDtypeStruct((TOK, 2048), bf), jax.ShapeDtypeStruct((TOK, 512), bf),
            jax.ShapeDtypeStruct((TOK, 512), bf),
        ) + tuple(jax.ShapeDtypeStruct((RANK, e - b), jnp.float32) for _, b, e in SPANS),
        in_specs=[VMEM] * 4,
        out_specs=(ANY,) * 3 + (VMEM,) * 4,
        scratch_shapes=[pltpu.SemaphoreType.DMA((3,))],
        compiler_params=pltpu.CompilerParams(vmem_limit_bytes=8 << 20),
        name="finish",
    )(dql, dkl, dvl, full)


def shards(q, k, v, do, hidden, lengths, qa, qb, va, vb):
    qg, dog, kg, vg = gather_call(q[0], do[0], k[0], v[0])
    dq, dk, dv = attend_call(lengths, qg, dog, kg, vg)
    landed = reduce_call(dq, dk, dv, hidden[0], qa, qb, va, vb)
    out = finish_call(*landed)
    return (out[0][None], out[1][None], out[2][None]) + tuple(out[3:])


def solution(mesh):
    token = P("dp", "ctx", None)
    return jax.shard_map(
        shards,
        mesh=mesh,
        in_specs=(token, token, token, token, token, P("dp", None), P(), P(), P(), P()),
        out_specs=(token, token, token, P(), P(), P(), P()),
        check_vma=False,
    )
```

time: 145 us -> 123 us (0.85)
  Pallas kernels: 132 us -> 117 us
  local copies, waits for them, and re-layouts: 11.4 us -> 4.55 us
    pallas_call x1, Pallas kernels: 36.8 us -> 1.73 us  [finish_call(): pl.pallas_call(finish_kernel, out_shape=(jax.ShapeDtypeStruct((TOK, 2048)...]
    pallas_call x1, Pallas kernels: 39.3 us -> 68.9 us  [reduce_call(): pl.pallas_call(reduce_kernel, out_shape=(jax.ShapeDtypeStruct((TOK, 2048)...]
    pallas_call x1, Pallas kernels: 19.8 us -> 12.3 us  [attend_call(): pl.pallas_call(attend_kernel, out_shape=(jax.ShapeDtypeStruct((512, 512),...]
    unnamed x37 -> x20, local copies, waits for them, and re-layouts: 11.4 us -> 4.55 us
    pallas_call x1, Pallas kernels: 36.3 us -> 34 us  [gather_call(): pl.pallas_call(gather_kernel, out_shape=(jax.ShapeDtypeStruct((512, 512),...]
where the time goes in v2:
time: 123 us; the launch traced here: 122 us
  Pallas kernels  117 us (95%)
  local copies, waits for them, and re-layouts  4.55 us (4%)
    pallas_call x1, Pallas kernels, reduce_call(): pl.pallas_call(reduce_kernel, out_shape=(jax.ShapeDtypeStruct((TOK, 2048)...  68.9 us
    pallas_call x1, Pallas kernels, gather_call(): pl.pallas_call(gather_kernel, out_shape=(jax.ShapeDtypeStruct((512, 512),...  34 us
    pallas_call x1, Pallas kernels, attend_call(): pl.pallas_call(attend_kernel, out_shape=(jax.ShapeDtypeStruct((512, 512),...  12.3 us
    unnamed x20, local copies, waits for them, and re-layouts  4.55 us

profile of v2, /device:TPU:1, one launch (start us, length us, event | category | flops | bytes accessed | tf_op | source)
XLA Modules:
  0.0 122.3 jit_solution(3981562462599288319)
XLA Ops:
  0.6 0.0 copy-start.1
  0.6 1.0 copy-done.1
  1.7 0.0 copy-start.2
  1.7 1.0 copy-done.2
  2.7 0.0 copy-start.3
  2.7 0.9 copy-done.3
  3.6 0.0 copy-start.4
  3.6 0.9 copy-done.4
  4.5 34.0 %gather.1 = (bf16[512,512]{1,0:T(8,128)(2,1)S(1)}, bf16[512,512]{1,0:T(8,128)(2,1)S(1)}, bf16[4096,128]{1,0:T(8,128)(2,1)S(1)}, bf16[4096,128]{1,0:T(8,128)(2,1)S(1)}) custom-call(bf16[128,2048]{1,0:T(8,128)(2,1)S(1)} %bitcast.9, bf16[128,2048]{1,0:T(8,128)(2,1)S(1)} %bitcast.10, bf16[128,512]{1,0:T(8,128)(2,1)S(1)} %bitcast.11, bf16[128,512]{1,0:T(8,128)(2,1)S(1)} %bitcast.12), custom_call_target="tpu_custom_call" | custom-call | tf_op jit(solution)/shard_map/gather/pallas_call | solution.py:179
  38.5 0.0 copy-start.9
  38.5 0.6 copy-done.9
  39.2 0.0 copy-start
  39.2 0.0 copy-start.5
  39.2 0.0 copy-start.6
  39.2 0.0 copy-start.7
  39.2 0.0 copy-start.8
  39.2 12.3 %attend.1 = (bf16[512,512]{1,0:T(8,128)(2,1)S(1)}, bf16[4096,128]{1,0:T(8,128)(2,1)S(1)}, bf16[4096,128]{1,0:T(8,128)(2,1)S(1)}) custom-call(s32[1,16]{1,0:T(1,128)S(1)} %copy-done.9, bf16[512,512]{1,0:T(8,128)(2,1)S(1)} %get-tuple-element.25.q_ref, bf16[512,512]{1,0:T(8,128)(2,1)S(1)} %get-tuple-element.26.do_ref, ...), custom_call_target="tpu_custom_call" | custom-call | tf_op jit(solution)/shard_map/attend/pallas_call | solution.py:298
  51.5 0.0 copy-done
  51.6 0.0 copy-done.5
  51.6 0.0 copy-done.6
  51.6 0.0 copy-done.7
  51.6 0.0 copy-done.8
  51.6 68.9 %reduce.1 = (bf16[128,2048]{1,0:T(8,128)(2,1)S(1)}, bf16[128,512]{1,0:T(8,128)(2,1)S(1)}, bf16[128,512]{1,0:T(8,128)(2,1)S(1)}, bf16[2,2,8,16,384]{4,3,2,1,0:T(8,128)(2,1)S(1)}) custom-call(bf16[512,512]{1,0:T(8,128)(2,1)S(1)} %get-tuple-element.29.dq_ref, bf16[4096,128]{1,0:T(8,128)(2,1)S(1)} %get-tuple-element.30.dk_ref, ...), custom_call_target="tpu_custom_call" | custom-call | tf_op jit(solution)/shard_map/reduce/pallas_call | solution.py:512
  120.5 1.7 %finish.1 = (bf16[128,2048]{1,0:T(8,128)(2,1)}, bf16[128,512]{1,0:T(8,128)(2,1)}, bf16[128,512]{1,0:T(8,128)(2,1)}, f32[16,4096]{1,0:T(8,128)}, f32[16,2048]{1,0...) custom-call(bf16[128,2048]{1,0:T(8,128)(2,1)S(1)} %get-tuple-element.32.dql_ref, ...), custom_call_target="tpu_custom_call" | custom-call | tf_op jit(solution)/shard_map/finish/pallas_call | solution.py:561
Async XLA Ops:
  0.6 1.0 copy-start.1
  1.7 1.0 copy-start.2
  2.7 0.9 copy-start.3
  3.6 0.9 copy-start.4
  38.5 0.7 copy-start.9
  39.2 12.4 %copy-start = (bf16[1,128,4096]{2,1,0:T(8,128)(2,1)S(1)}, bf16[1,128,4096]{2,1,0:T(8,128)(2,1)}, u32[]{:S(2)}) copy-start(bf16[1,128,4096]{2,1,0:T(8,128)(2,1)} %param.14) | copy-start | bytes 3145732
  39.2 12.4 %copy-start.5 = (bf16[16,4096]{1,0:T(8,128)(2,1)S(1)}, bf16[16,4096]{1,0:T(8,128)(2,1)}, u32[]{:S(2)}) copy-start(bf16[16,4096]{1,0:T(8,128)(2,1)} %qa_ref.1) | copy-start | bytes 393220
  39.2 12.4 %copy-start.6 = (bf16[16,4096]{1,0:T(8,128)(2,1)S(1)}, bf16[16,4096]{1,0:T(8,128)(2,1)}, u32[]{:S(2)}) copy-start(bf16[16,4096]{1,0:T(8,128)(2,1)} %va_ref.1) | copy-start | bytes 393220
  39.2 12.4 %copy-start.7 = (bf16[16,2048]{1,0:T(8,128)(2,1)S(1)}, bf16[16,2048]{1,0:T(8,128)(2,1)}, u32[]{:S(2)}) copy-start(bf16[16,2048]{1,0:T(8,128)(2,1)} %qb_ref.1) | copy-start | bytes 196612
  39.2 12.4 %copy-start.8 = (bf16[16,512]{1,0:T(8,128)(2,1)S(1)}, bf16[16,512]{1,0:T(8,128)(2,1)}, u32[]{:S(2)}) copy-start(bf16[16,512]{1,0:T(8,128)(2,1)} %vb_ref.1) | copy-start | bytes 49156

commit v3 on v2

--- a/solution.py
+++ b/solution.py
@@ -28,7 +28,7 @@
 LOG2E = math.log2(math.e)
 ANY = pl.BlockSpec(memory_space=pl.ANY)
 VMEM = pl.BlockSpec(memory_space=pltpu.VMEM)
-SMEM = pl.BlockSpec(memory_space=pltpu.SMEM)
+HBM = pl.BlockSpec(memory_space=pltpu.HBM)
 
 
 def nn(left, right):
@@ -182,7 +182,7 @@
             jax.ShapeDtypeStruct((512, 512), bf), jax.ShapeDtypeStruct((512, 512), bf),
             jax.ShapeDtypeStruct((SEQ, HEAD), bf), jax.ShapeDtypeStruct((SEQ, HEAD), bf),
         ),
-        in_specs=[ANY, ANY, VMEM, VMEM],
+        in_specs=[HBM] * 4,
         out_specs=(VMEM,) * 4,
         scratch_shapes=[
             pltpu.VMEM((SEQ, HEAD), bf), pltpu.VMEM((SEQ, HEAD), bf),
@@ -195,8 +195,10 @@
     )(q, do, k, v)
 
 
-def attend_kernel(len_ref, q_ref, do_ref, k_ref, v_ref, dq_ref, dk_ref, dv_ref,
-                  s_ref, kt, vt, qs, dos, dot_ref, ot, dqt, dka, dva):
+def attend_kernel(len_hbm, q_ref, do_ref, k_ref, v_ref, dq_ref, dk_ref, dv_ref,
+                  s_ref, kt, vt, qs, dos, dot_ref, ot, dqt, dka, dva, len_ref, sem):
+    lengths = pltpu.make_async_copy(len_hbm, len_ref, sem)
+    lengths.start()
     _, z, _ = place()
     bf, f32 = jnp.bfloat16, jnp.float32
     fold = SCALE * LOG2E
@@ -210,6 +212,7 @@
         return carry
 
     lax.fori_loop(0, NKB, prepare, 0)
+    lengths.wait()
     starts = [jnp.int32(0)]
     for d in range(DOCS - 1):
         starts.append(starts[-1] + len_ref[0, d])
@@ -301,7 +304,7 @@
             jax.ShapeDtypeStruct((512, 512), bf),
             jax.ShapeDtypeStruct((SEQ, HEAD), bf), jax.ShapeDtypeStruct((SEQ, HEAD), bf),
         ),
-        in_specs=[SMEM, VMEM, VMEM, VMEM, VMEM],
+        in_specs=[HBM, VMEM, VMEM, VMEM, VMEM],
         out_specs=(VMEM, VMEM, VMEM),
         scratch_shapes=[
             pltpu.VMEM((NKB, KB, WIDE), f32),
@@ -309,6 +312,7 @@
             pltpu.VMEM((WIDE, HEAD), bf), pltpu.VMEM((WIDE, HEAD), bf),
             pltpu.VMEM((HEAD, WIDE), f32), pltpu.VMEM((HEAD, WIDE), f32), pltpu.VMEM((HEAD, WIDE), f32),
             pltpu.VMEM((NKB, KB, HEAD), f32), pltpu.VMEM((NKB, KB, HEAD), f32),
+            pltpu.SMEM((1, DOCS), jnp.int32), pltpu.SemaphoreType.DMA,
         ],
         compiler_params=pltpu.CompilerParams(vmem_limit_bytes=46 << 20),
         name="attend",
@@ -326,7 +330,7 @@
     own = 2 * a + c
     peers = group_peers(a, c)
     ways = (1, -1)
-    chunks = ((dk_ref, 1 - a), (dv_ref, 1 - a), (dk_ref, a), (dv_ref, a))
+    chunks = ((dv_ref, 1 - a), (dv_ref, a), (dk_ref, 1 - a), (dk_ref, a))
     head_cols = pl.ds(mult(own * HEAD, HEAD), HEAD)
     wide_cols = pl.ds(mult(own * 512, 512), 512)
     seat = lax.axis_index("dp") * 2 + a
@@ -357,7 +361,7 @@
         return (w * 4 + d - 1) * 4 + j
 
     def starts_far(w, j):
-        return (j < 2) == (w == 0)
+        return (j % 2 == 0) == (w == 0)
 
     def send_on(w, d, j, src):
         k = at(w, d, j)
@@ -417,24 +421,15 @@
         came(full.at[u, 1 - c], s5.at[u], r5.at[u], sibling)
         full_out[u] = full[u]
 
-    for j in range(4):
-        for w in (0, 1):
-            if starts_far(w, j):
-                send_on(w, 4, j, chunks[j][0].at[rows_of(j, 4)])
-    for j in range(4):
-        for w in (0, 1):
-            if not starts_far(w, j):
-                send_on(w, 3, j, chunks[j][0].at[rows_of(j, 3 * ways[w])])
-    for p, (pa, pc) in enumerate(peers):
-        go(dq_ref.at[pl.ds(mult((2 * pa + pc) * TOK, TOK), TOK)], dql.at[:, wide_cols],
-           xs.at[p], xr.at[p], ids[p])
-    hidden = hid_ref[...]
-    query_proj = nt(qa_ref[...], hidden).astype(bf)
-    value_proj = nt(va_ref[...], hidden).astype(bf)
-    part[1, :, 4608:PACKED] = jnp.zeros((RANK, PACKED - 4608), bf)
-
-    def forward(d):
-        for j in range(4):
+    def first_sends(js):
+        for d, far in ((4, True), (3, False)):
+            for j in js:
+                for w in (0, 1):
+                    if starts_far(w, j) == far:
+                        send_on(w, d, j, chunks[j][0].at[rows_of(j, d * ways[w])])
+
+    def forward(d, js):
+        for j in js:
             for w in (0, 1):
                 if d == 3 and not starts_far(w, j):
                     continue
@@ -444,63 +439,72 @@
                 rb[slot] = (rb[slot].astype(f32) + own_part).astype(bf)
                 send_on(w, d, j, rb.at[slot])
 
-    forward(3)
+    def last(i, dst):
+        for j in (2 * i, 2 * i + 1):
+            for w in (0, 1):
+                arrived(w, 1, j)
+            both = rb[at(0, 1, j)].astype(f32) + rb[at(1, 1, j)].astype(f32)
+            fin[j] = (both + chunks[j][0][rows_of(j, 0), :].astype(f32)).astype(bf)
+            for p in ((1, 2) if j % 2 == 0 else (0,)):
+                go(fin.at[j, pl.ds(mult(peers[p][1] * TOK, TOK), TOK)], dst.at[:, head_cols],
+                   gs.at[2 * p + i], gr.at[2 * p + i], ids[p])
+        one = pltpu.make_async_copy(
+            fin.at[2 * i + 1, pl.ds(mult(c * TOK, TOK), TOK)], dst.at[:, head_cols], ls.at[1 + i])
+        one.start()
+        return one
+
+    def returned(i, dst, own_copy):
+        own_copy.wait()
+        for p, (pa, pc) in enumerate(peers):
+            cols = pl.ds(mult((2 * pa + pc) * HEAD, HEAD), HEAD)
+            came(dst.at[:, cols], gs.at[2 * p + i], gr.at[2 * p + i], ids[p])
+
+    values, keys = (0, 1), (2, 3)
+    first_sends(values)
+    for p, (pa, pc) in enumerate(peers):
+        go(dq_ref.at[pl.ds(mult((2 * pa + pc) * TOK, TOK), TOK)], dql.at[:, wide_cols],
+           xs.at[p], xr.at[p], ids[p])
+    hidden = hid_ref[...]
+    query_proj = nt(qa_ref[...], hidden).astype(bf)
+    value_proj = nt(va_ref[...], hidden).astype(bf)
+    part[1, :, 4608:PACKED] = jnp.zeros((RANK, PACKED - 4608), bf)
+    forward(3, values)
+    forward(2, values)
+    forward(1, values)
+    first_sends(keys)
+    own_values = last(0, dvl)
     mine.wait()
     for p, (pa, pc) in enumerate(peers):
         cols = pl.ds(mult((2 * pa + pc) * 512, 512), 512)
         came(dql.at[:, cols], xs.at[p], xr.at[p], ids[p])
     query = dql[...]
-    dql_out[...] = query
     part[0, :, 4096:6144] = (2.0 * nn(query_proj, query)).astype(bf)
     query_low = nt(qb_ref[...], query).astype(bf)
     part[0, :, 0:4096] = (2.0 * nn(query_low, hidden)).astype(bf)
     core_send(0)
-    forward(2)
-    z_send(0)
-    forward(1)
-    seat_send(0)
-    for j in range(4):
-        for w in (0, 1):
-            arrived(w, 1, j)
-        both = rb[at(0, 1, j)].astype(f32) + rb[at(1, 1, j)].astype(f32)
-        fin[j] = (both + chunks[j][0][rows_of(j, 0), :].astype(f32)).astype(bf)
-        if j == 1:
-            for i, dst in ((1, dvl), (0, dkl)):
-                for p in (1, 2):
-                    go(fin.at[i, pl.ds(mult(peers[p][1] * TOK, TOK), TOK)], dst.at[:, head_cols],
-                       gs.at[2 * p + i], gr.at[2 * p + i], ids[p])
-    keep = []
-    for i, dst in ((1, dvl), (0, dkl)):
-        go(fin.at[2 + i, pl.ds(mult((1 - c) * TOK, TOK), TOK)], dst.at[:, head_cols],
-           gs.at[i], gr.at[i], ids[0])
-        one = pltpu.make_async_copy(
-            fin.at[2 + i, pl.ds(mult(c * TOK, TOK), TOK)], dst.at[:, head_cols], ls.at[1 + i])
-        one.start()
-        keep.append(one)
-    for one in keep:
-        one.wait()
-
-    def returned(i, dst):
-        for p, (pa, pc) in enumerate(peers):
-            cols = pl.ds(mult((2 * pa + pc) * HEAD, HEAD), HEAD)
-            came(dst.at[:, cols], gs.at[2 * p + i], gr.at[2 * p + i], ids[p])
-
-    returned(1, dvl)
+    forward(3, keys)
+    returned(0, dvl, own_values)
     value = dvl[...]
     part[1, :, 4096:4608] = (2.0 * nn(value_proj, value)).astype(bf)
     value_low = nt(vb_ref[...], value).astype(bf)
     part[1, :, 0:4096] = (2.0 * nn(value_low, hidden)).astype(bf)
     core_send(1)
+    z_send(0)
+    z_send(1)
+    forward(2, keys)
+    seat_send(0)
+    seat_send(1)
+    forward(1, keys)
+    dql_out[...] = query
     dvl_out[...] = value
-    z_send(1)
     z_spread(0)
-    seat_send(1)
+    own_keys = last(1, dkl)
+    z_spread(1)
     core_spread(0)
-    returned(0, dkl)
+    returned(1, dkl, own_keys)
     dkl_out[...] = dkl[...]
-    z_spread(1)
+    core_spread(1)
     collect(0)
-    core_spread(1)
     collect(1)
     for one in sent:
         one.wait_send()

time: 123 us -> 117 us (0.951)
  Pallas kernels: 117 us -> 112 us
    pallas_call x1, Pallas kernels: 68.9 us -> 64.3 us  [reduce_call(): pl.pallas_call(reduce_kernel, out_shape=(jax.ShapeDtypeStruct((TOK, 2048)...]
where the time goes in v3:
time: 117 us
  Pallas kernels  112 us (96%)
  local copies, waits for them, and re-layouts  4.55 us (4%)
    pallas_call x1, Pallas kernels, reduce_call(): pl.pallas_call(reduce_kernel, out_shape=(jax.ShapeDtypeStruct((TOK, 2048)...  64.3 us
    pallas_call x1, Pallas kernels, gather_call(): pl.pallas_call(gather_kernel, out_shape=(jax.ShapeDtypeStruct((512, 512),...  34 us
    pallas_call x1, Pallas kernels, attend_call(): pl.pallas_call(attend_kernel, out_shape=(jax.ShapeDtypeStruct((512, 512),...  11.8 us
    unnamed x20, local copies, waits for them, and re-layouts  4.55 us

profile of v3, /device:TPU:1, one launch (start us, length us, event | category | flops | bytes accessed | tf_op | source)
XLA Modules:
  0.0 117.2 jit_solution(18171892083847179300)
XLA Ops:
  0.6 0.0 copy-start.1
  0.6 1.0 copy-done.1
  1.7 0.0 copy-start.2
  1.7 1.0 copy-done.2
  2.7 0.0 copy-start.3
  2.7 0.9 copy-done.3
  3.6 0.0 copy-start.4
  3.6 0.9 copy-done.4
  4.5 34.0 %gather.1 = (bf16[512,512]{1,0:T(8,128)(2,1)S(1)}, bf16[512,512]{1,0:T(8,128)(2,1)S(1)}, bf16[4096,128]{1,0:T(8,128)(2,1)S(1)}, bf16[4096,128]{1,0:T(8,128)(2,1)S(1)}) custom-call(bf16[128,2048]{1,0:T(8,128)(2,1)S(1)} %bitcast.9, bf16[128,2048]{1,0:T(8,128)(2,1)S(1)} %bitcast.10, bf16[128,512]{1,0:T(8,128)(2,1)S(1)} %bitcast.11, bf16[128,512]{1,0:T(8,128)(2,1)S(1)} %bitcast.12), custom_call_target="tpu_custom_call" | custom-call | tf_op jit(solution)/shard_map/gather/pallas_call | solution.py:179
  38.5 0.0 copy-start.9
  38.5 0.6 copy-done.9
  39.2 0.0 copy-start
  39.2 0.0 copy-start.5
  39.2 0.0 copy-start.6
  39.2 0.0 copy-start.7
  39.2 0.0 copy-start.8
  39.2 11.8 %attend.1 = (bf16[512,512]{1,0:T(8,128)(2,1)S(1)}, bf16[4096,128]{1,0:T(8,128)(2,1)S(1)}, bf16[4096,128]{1,0:T(8,128)(2,1)S(1)}) custom-call(s32[1,16]{1,0:T(1,128)S(1)} %copy-done.9, bf16[512,512]{1,0:T(8,128)(2,1)S(1)} %get-tuple-element.25.q_ref, bf16[512,512]{1,0:T(8,128)(2,1)S(1)} %get-tuple-element.26.do_ref, ...), custom_call_target="tpu_custom_call" | custom-call | tf_op jit(solution)/shard_map/attend/pallas_call | solution.py:301
  51.1 0.0 copy-done
  51.1 0.0 copy-done.5
  51.1 0.0 copy-done.6
  51.1 0.0 copy-done.7
  51.1 0.0 copy-done.8
  51.1 64.3 %reduce.1 = (bf16[128,2048]{1,0:T(8,128)(2,1)S(1)}, bf16[128,512]{1,0:T(8,128)(2,1)S(1)}, bf16[128,512]{1,0:T(8,128)(2,1)S(1)}, bf16[2,2,8,16,384]{4,3,2,1,0:T(8,128)(2,1)S(1)}) custom-call(bf16[512,512]{1,0:T(8,128)(2,1)S(1)} %get-tuple-element.29.dq_ref, bf16[4096,128]{1,0:T(8,128)(2,1)S(1)} %get-tuple-element.30.dk_ref, ...), custom_call_target="tpu_custom_call" | custom-call | tf_op jit(solution)/shard_map/reduce/pallas_call | solution.py:516
  115.4 1.7 %finish.1 = (bf16[128,2048]{1,0:T(8,128)(2,1)}, bf16[128,512]{1,0:T(8,128)(2,1)}, bf16[128,512]{1,0:T(8,128)(2,1)}, f32[16,4096]{1,0:T(8,128)}, f32[16,2048]{1,0...) custom-call(bf16[128,2048]{1,0:T(8,128)(2,1)S(1)} %get-tuple-element.32.dql_ref, ...), custom_call_target="tpu_custom_call" | custom-call | tf_op jit(solution)/shard_map/finish/pallas_call | solution.py:565
Async XLA Ops:
  0.6 1.0 copy-start.1
  1.7 1.0 copy-start.2
  2.7 0.9 copy-start.3
  3.6 0.9 copy-start.4
  38.5 0.7 copy-start.9
  39.2 11.9 %copy-start = (bf16[1,128,4096]{2,1,0:T(8,128)(2,1)S(1)}, bf16[1,128,4096]{2,1,0:T(8,128)(2,1)}, u32[]{:S(2)}) copy-start(bf16[1,128,4096]{2,1,0:T(8,128)(2,1)} %param.14) | copy-start | bytes 3145732
  39.2 11.9 %copy-start.5 = (bf16[16,4096]{1,0:T(8,128)(2,1)S(1)}, bf16[16,4096]{1,0:T(8,128)(2,1)}, u32[]{:S(2)}) copy-start(bf16[16,4096]{1,0:T(8,128)(2,1)} %qa_ref.1) | copy-start | bytes 393220
  39.2 11.9 %copy-start.6 = (bf16[16,4096]{1,0:T(8,128)(2,1)S(1)}, bf16[16,4096]{1,0:T(8,128)(2,1)}, u32[]{:S(2)}) copy-start(bf16[16,4096]{1,0:T(8,128)(2,1)} %va_ref.1) | copy-start | bytes 393220
  39.2 11.9 %copy-start.7 = (bf16[16,2048]{1,0:T(8,128)(2,1)S(1)}, bf16[16,2048]{1,0:T(8,128)(2,1)}, u32[]{:S(2)}) copy-start(bf16[16,2048]{1,0:T(8,128)(2,1)} %qb_ref.1) | copy-start | bytes 196612
  39.2 11.9 %copy-start.8 = (bf16[16,512]{1,0:T(8,128)(2,1)S(1)}, bf16[16,512]{1,0:T(8,128)(2,1)}, u32[]{:S(2)}) copy-start(bf16[16,512]{1,0:T(8,128)(2,1)} %vb_ref.1) | copy-start | bytes 49156

commit v4 on v3

--- a/solution.py
+++ b/solution.py
@@ -17,6 +17,8 @@
 SEQ = 4096
 KB = 256
 WIDE = GROUP * CHIP_ROWS
+PAIRS = SEQ // KB + HALF_SEQ // KB
+FOLD = HEAD ** (-0.5) * math.log2(math.e)
 NKB = SEQ // KB
 RANK = 16
 PACKED = 6144
@@ -25,9 +27,9 @@
 DOCS = 16
 NEG = -1e30
 SCALE = HEAD ** (-0.5)
-LOG2E = math.log2(math.e)
 ANY = pl.BlockSpec(memory_space=pl.ANY)
 VMEM = pl.BlockSpec(memory_space=pltpu.VMEM)
+SMEM = pl.BlockSpec(memory_space=pltpu.SMEM)
 HBM = pl.BlockSpec(memory_space=pltpu.HBM)
 
 
@@ -76,8 +78,17 @@
     return ids
 
 
-def gather_kernel(q_ref, do_ref, k_ref, v_ref, qg_ref, dog_ref, kg_ref, vg_ref,
-                  kall, vall, qall, doall, gs, gr, xs, xr, rs, rr, ls):
+def doc_starts(len_ref):
+    starts = [jnp.int32(0)]
+    for d in range(DOCS - 1):
+        starts.append(starts[-1] + len_ref[0, d])
+    return starts
+
+
+def gather_kernel(len_ref, q_ref, do_ref, k_ref, v_ref,
+                  qs, dog_ref, kg_ref, vg_ref, e_ref, top_ref, max_ref, sum_ref, ot,
+                  kall, vall, qall, doall, begin_ref, gs, gr, xs, xr, rs, rr, ls):
+    bf, f32 = jnp.bfloat16, jnp.float32
     a, z, c = place()
     ids = ring_and_group(a, z, c)
     own = 2 * a + c
@@ -103,8 +114,8 @@
                         gs.at[2 * p + i], gr.at[2 * p + i], ids[p])
             cp.start()
             sent.append(cp)
-    for p, (pa, pc) in enumerate(peers):
-        for i, (src, dst) in enumerate(((q_ref, qall), (do_ref, doall))):
+    for i, (src, dst) in enumerate(((q_ref, qall), (do_ref, doall))):
+        for p, (pa, pc) in enumerate(peers):
             head = 2 * pa + pc
             cp = remote(src.at[:, pl.ds(mult(head * 512, 512), 512)],
                         dst.at[pl.ds(mult(own * TOK, TOK), TOK)],
@@ -141,81 +152,145 @@
     def carries(w, s, j):
         return s < 3 or (j < 2) == (w == 0)
 
+    def position(t):
+        return t * HALF_SEQ + z * CHIP_ROWS + lax.broadcasted_iota(jnp.int32, (1, WIDE), 1) % CHIP_ROWS
+
+    def fold_in(t, y, zz, diagonal=False):
+        first = y * HALF_SEQ + zz * CHIP_ROWS
+        rows = pl.ds(mult(first, CHIP_ROWS), CHIP_ROWS)
+        slot = t * RING + y * RING + zz
+        key_pos = lax.broadcasted_iota(jnp.int32, (KB, WIDE), 0)
+        visible = key_pos >= begin_ref[t] - first
+        if diagonal:
+            visible = visible & (key_pos <= position(t) - first)
+        s = jnp.where(visible, nt(kall[rows, :], qs[t]), NEG)
+        old = max_ref[t]
+        new = jnp.maximum(old, jnp.max(s, axis=0, keepdims=True) * FOLD)
+        e = jnp.exp2(s * FOLD - new)
+        factor = jnp.exp2(old - new)
+        sum_ref[t] = sum_ref[t] * factor + jnp.sum(e, axis=0, keepdims=True)
+        eb = e.astype(bf)
+        e_ref[slot] = eb
+        top_ref[slot] = new
+        max_ref[t] = new
+        ot[t] = ot[t] * factor + nn(vall[rows, :].T, eb)
+
+    def fold_both(y, s, w):
+        zz = (z + 2 * RING - ways[w] * (s + 1)) % RING
+
+        def one(t, carry):
+            @pl.when(y * RING + zz <= t * RING + z)
+            def _():
+                fold_in(t, y, zz)
+
+            return carry
+
+        lax.fori_loop(0, 2, one, 0)
+
+    def relay(s, half):
+        for w in (0, 1):
+            for j in (2 * half, 2 * half + 1):
+                if carries(w, s, j):
+                    arrived(w, s, j)
+                    if s < 3 and carries(w, s + 1, j):
+                        send_on(w, s + 1, j)
+            if s > 0 and carries(w, s, 2 * half):
+                fold_both(1 - a if half else a, s, w)
+
     for one in local:
         one.wait()
     group_arrived(0)
     for j in (0, 1):
         for w in (0, 1):
             send_on(w, 0, j)
+    starts = doc_starts(len_ref)
+    for t in range(2):
+        begin = jnp.zeros((1, WIDE), jnp.int32)
+        for at_start in starts:
+            begin = jnp.where(at_start <= position(t), jnp.maximum(begin, at_start), begin)
+        begin_ref[t] = begin
+        max_ref[t] = jnp.full((1, WIDE), NEG, f32)
+        sum_ref[t] = jnp.zeros((1, WIDE), f32)
+        ot[t] = jnp.zeros((HEAD, WIDE), f32)
     group_arrived(1)
     group_arrived(2)
     for j in (2, 3):
         for w in (0, 1):
             send_on(w, 0, j)
-    for s in range(4):
-        for j in range(4):
-            for w in (0, 1):
-                if carries(w, s, j):
-                    arrived(w, s, j)
-                    if s < 3 and carries(w, s + 1, j):
-                        send_on(w, s + 1, j)
+    relay(0, 0)
+
+    def crossed(i, dst):
+        wide[i].wait()
+        for p, (pa, pc) in enumerate(peers):
+            rows = pl.ds(mult((2 * pa + pc) * TOK, TOK), TOK)
+            remote(dst.at[rows], dst.at[rows], xs.at[2 * p + i], xr.at[2 * p + i], ids[p]).wait_recv()
+
+    crossed(0, qall)
+    for t in range(2):
+        for h in range(GROUP):
+            qs[t, h * CHIP_ROWS:(h + 1) * CHIP_ROWS, :] = qall[
+                t * CHIP_ROWS:(t + 1) * CHIP_ROWS, h * HEAD:(h + 1) * HEAD]
+    relay(0, 1)
+
+    def own_tile(t, carry):
+        fold_in(t, t, z, True)
+        return carry
+
+    lax.fori_loop(0, 2, own_tile, 0)
+    fold_in(1, 0, z)
+    for half in (0, 1):
+        for w in (0, 1):
+            fold_both(1 - a if half else a, 0, w)
+        relay(1, half)
+    for s in (2, 3):
+        for half in (0, 1):
+            relay(s, half)
     kg_ref[...] = kall[...]
     vg_ref[...] = vall[...]
-    for one in wide:
-        one.wait()
-    for p, (pa, pc) in enumerate(peers):
-        rows = pl.ds(mult((2 * pa + pc) * TOK, TOK), TOK)
-        for i, dst in enumerate((qall, doall)):
-            remote(dst.at[rows], dst.at[rows], xs.at[2 * p + i], xr.at[2 * p + i], ids[p]).wait_recv()
-    qg_ref[...] = qall[...]
+    crossed(1, doall)
     dog_ref[...] = doall[...]
     for one in sent:
         one.wait_send()
 
 
-def gather_call(q, do, k, v):
-    bf = jnp.bfloat16
+def gather_call(lengths, q, do, k, v):
+    bf, f32 = jnp.bfloat16, jnp.float32
     dma = pltpu.SemaphoreType.DMA
     return pl.pallas_call(
         gather_kernel,
         out_shape=(
-            jax.ShapeDtypeStruct((512, 512), bf), jax.ShapeDtypeStruct((512, 512), bf),
+            jax.ShapeDtypeStruct((2, WIDE, HEAD), bf), jax.ShapeDtypeStruct((512, 512), bf),
             jax.ShapeDtypeStruct((SEQ, HEAD), bf), jax.ShapeDtypeStruct((SEQ, HEAD), bf),
+            jax.ShapeDtypeStruct((PAIRS, KB, WIDE), bf), jax.ShapeDtypeStruct((PAIRS, 1, WIDE), f32),
+            jax.ShapeDtypeStruct((2, 1, WIDE), f32), jax.ShapeDtypeStruct((2, 1, WIDE), f32),
+            jax.ShapeDtypeStruct((2, HEAD, WIDE), f32),
         ),
-        in_specs=[HBM] * 4,
-        out_specs=(VMEM,) * 4,
+        in_specs=[SMEM] + [HBM] * 4,
+        out_specs=(VMEM,) * 9,
         scratch_shapes=[
             pltpu.VMEM((SEQ, HEAD), bf), pltpu.VMEM((SEQ, HEAD), bf),
-            pltpu.VMEM((512, 512), bf), pltpu.VMEM((512, 512), bf),
+            pltpu.VMEM((512, 512), bf), pltpu.VMEM((512, 512), bf), pltpu.VMEM((2, 1, WIDE), jnp.int32),
             dma((6,)), dma((6,)), dma((6,)), dma((6,)), dma((32,)), dma((32,)), dma((4,)),
         ],
         compiler_params=pltpu.CompilerParams(
-            collective_id=0, has_side_effects=True, vmem_limit_bytes=14 << 20),
+            collective_id=0, has_side_effects=True, vmem_limit_bytes=26 << 20),
         name="gather",
-    )(q, do, k, v)
-
-
-def attend_kernel(len_hbm, q_ref, do_ref, k_ref, v_ref, dq_ref, dk_ref, dv_ref,
-                  s_ref, kt, vt, qs, dos, dot_ref, ot, dqt, dka, dva, len_ref, sem):
-    lengths = pltpu.make_async_copy(len_hbm, len_ref, sem)
-    lengths.start()
+    )(lengths, q, do, k, v)
+
+
+def attend_kernel(len_ref, q_ref, do_ref, k_ref, v_ref, e_ref, top_ref, max_ref, sum_ref, ot_ref,
+                  dq_ref, dk_ref, dv_ref, kt, dos, dot_ref, dqt, dka, dva):
     _, z, _ = place()
     bf, f32 = jnp.bfloat16, jnp.float32
-    fold = SCALE * LOG2E
 
     def prepare(b, carry):
-        rows = pl.ds(mult(b * KB, KB), KB)
-        kt[b] = k_ref[rows, :].T
-        vt[b] = v_ref[rows, :].T
+        kt[b] = k_ref[pl.ds(mult(b * KB, KB), KB), :].T
         dka[b] = jnp.zeros((KB, HEAD), f32)
         dva[b] = jnp.zeros((KB, HEAD), f32)
         return carry
 
     lax.fori_loop(0, NKB, prepare, 0)
-    lengths.wait()
-    starts = [jnp.int32(0)]
-    for d in range(DOCS - 1):
-        starts.append(starts[-1] + len_ref[0, d])
+    starts = doc_starts(len_ref)
 
     def tile(t, carry):
         first = t * HALF_SEQ + z * CHIP_ROWS
@@ -223,62 +298,30 @@
         for h in range(GROUP):
             part = slice(h * HEAD, (h + 1) * HEAD)
             stack = slice(h * CHIP_ROWS, (h + 1) * CHIP_ROWS)
-            qs[stack, :] = q_ref[rows, part]
             grads = do_ref[rows, part]
             dos[stack, :] = grads
             dot_ref[:, stack] = grads.astype(f32).T
-        query_pos = first + lax.broadcasted_iota(jnp.int32, (1, WIDE), 1) % CHIP_ROWS
-        begin = jnp.zeros((1, WIDE), jnp.int32)
-        low, high = jnp.int32(0), jnp.int32(0)
+        low = jnp.int32(0)
         for at in starts:
-            begin = jnp.where(at <= query_pos, jnp.maximum(begin, at), begin)
             low = jnp.where(at <= first, jnp.maximum(low, at), low)
-            high = jnp.where(at < first + CHIP_ROWS, jnp.maximum(high, at), high)
-        kb0 = low // KB
-        kb1 = first // KB + 1
-        kbm = jnp.minimum((high + KB - 1) // KB, kb1 - 1)
-
-        def score(b, top):
-            keys = k_ref[pl.ds(mult(b * KB, KB), KB), :]
-            s = nt(keys, qs[...])
-            s_ref[b] = s
-            return jnp.maximum(top, jnp.max(s, axis=0, keepdims=True))
-
-        def score_masked(b, top):
-            keys = k_ref[pl.ds(mult(b * KB, KB), KB), :]
-            s = nt(keys, qs[...])
-            key_pos = b * KB + lax.broadcasted_iota(jnp.int32, (KB, WIDE), 0)
-            s = jnp.where((key_pos >= begin) & (key_pos <= query_pos), s, NEG)
-            s_ref[b] = s
-            return jnp.maximum(top, jnp.max(s, axis=0, keepdims=True))
-
-        top = score_masked(kb1 - 1, jnp.full((1, WIDE), NEG, f32))
-        top = lax.fori_loop(kb0, kbm, score_masked, top)
-        top = lax.fori_loop(kbm, kb1 - 1, score, top) * fold
-        ot[...] = jnp.zeros_like(ot)
-
-        def weigh(b, total):
-            e = jnp.exp2(s_ref[b] * fold - top)
-            s_ref[b] = e
-            ot[...] += nn(vt[b], e.astype(bf))
-            return total + jnp.sum(e, axis=0, keepdims=True)
-
-        total = lax.fori_loop(kb0, kb1, weigh, jnp.zeros((1, WIDE), f32))
-        inverse = 1.0 / total
-        delta = jnp.sum(dot_ref[...] * ot[...], axis=0, keepdims=True) * inverse
+        inverse = 1.0 / sum_ref[t]
+        top = max_ref[t]
+        delta = jnp.sum(dot_ref[...] * ot_ref[t], axis=0, keepdims=True) * inverse
         dqt[...] = jnp.zeros_like(dqt)
 
         def back(b, carry):
+            slot = t * RING + b
             values = v_ref[pl.ds(mult(b * KB, KB), KB), :]
-            p = s_ref[b] * inverse
+            factor = jnp.exp2(top_ref[slot] - top) * inverse
+            p = e_ref[slot].astype(f32) * factor
             gp = nt(values, dos[...])
             ds = (p * (gp - delta)).astype(bf)
             dva[b] += nn(p.astype(bf), dos[...])
-            dka[b] += nn(ds, qs[...])
+            dka[b] += nn(ds, q_ref[t])
             dqt[...] += nn(kt[b], ds)
             return carry
 
-        lax.fori_loop(kb0, kb1, back, 0)
+        lax.fori_loop(low // KB, first // KB + 1, back, 0)
         for h in range(GROUP):
             part = slice(h * HEAD, (h + 1) * HEAD)
             stack = slice(h * CHIP_ROWS, (h + 1) * CHIP_ROWS)
@@ -296,7 +339,7 @@
     lax.fori_loop(0, NKB, finish, 0)
 
 
-def attend_call(lengths, q, do, k, v):
+def attend_call(lengths, gathered):
     bf, f32 = jnp.bfloat16, jnp.float32
     return pl.pallas_call(
         attend_kernel,
@@ -304,19 +347,16 @@
             jax.ShapeDtypeStruct((512, 512), bf),
             jax.ShapeDtypeStruct((SEQ, HEAD), bf), jax.ShapeDtypeStruct((SEQ, HEAD), bf),
         ),
-        in_specs=[HBM, VMEM, VMEM, VMEM, VMEM],
-        out_specs=(VMEM, VMEM, VMEM),
+        in_specs=[SMEM] + [VMEM] * 9,
+        out_specs=(VMEM,) * 3,
         scratch_shapes=[
-            pltpu.VMEM((NKB, KB, WIDE), f32),
-            pltpu.VMEM((NKB, HEAD, KB), bf), pltpu.VMEM((NKB, HEAD, KB), bf),
-            pltpu.VMEM((WIDE, HEAD), bf), pltpu.VMEM((WIDE, HEAD), bf),
-            pltpu.VMEM((HEAD, WIDE), f32), pltpu.VMEM((HEAD, WIDE), f32), pltpu.VMEM((HEAD, WIDE), f32),
+            pltpu.VMEM((NKB, HEAD, KB), bf), pltpu.VMEM((WIDE, HEAD), bf),
+            pltpu.VMEM((HEAD, WIDE), f32), pltpu.VMEM((HEAD, WIDE), f32),
             pltpu.VMEM((NKB, KB, HEAD), f32), pltpu.VMEM((NKB, KB, HEAD), f32),
-            pltpu.SMEM((1, DOCS), jnp.int32), pltpu.SemaphoreType.DMA,
         ],
-        compiler_params=pltpu.CompilerParams(vmem_limit_bytes=46 << 20),
+        compiler_params=pltpu.CompilerParams(vmem_limit_bytes=20 << 20),
         name="attend",
-    )(lengths, q, do, k, v)
+    )(lengths, *gathered)
 
 
 def reduce_kernel(dq_ref, dk_ref, dv_ref, hid_ref, qa_ref, qb_ref, va_ref, vb_ref,
@@ -577,8 +617,8 @@
 
 
 def shards(q, k, v, do, hidden, lengths, qa, qb, va, vb):
-    qg, dog, kg, vg = gather_call(q[0], do[0], k[0], v[0])
-    dq, dk, dv = attend_call(lengths, qg, dog, kg, vg)
+    gathered = gather_call(lengths, q[0], do[0], k[0], v[0])
+    dq, dk, dv = attend_call(lengths, gathered)
     landed = reduce_call(dq, dk, dv, hidden[0], qa, qb, va, vb)
     out = finish_call(*landed)
     return (out[0][None], out[1][None], out[2][None]) + tuple(out[3:])

time: 117 us -> 113 us (0.966)
  Pallas kernels: 112 us -> 106 us
    pallas_call x1, Pallas kernels: 64.3 us -> 54.9 us  [reduce_call(): pl.pallas_call(reduce_kernel, out_shape=(jax.ShapeDtypeStruct((TOK, 2048)...]
    pallas_call x1, Pallas kernels: 34 us -> 39.5 us  [gather_call(): pl.pallas_call(gather_kernel, out_shape=(jax.ShapeDtypeStruct((2, WIDE, H...]
    pallas_call x1, Pallas kernels: 11.8 us -> 9.76 us  [attend_call(): pl.pallas_call(attend_kernel, out_shape=(jax.ShapeDtypeStruct((512, 512),...]
    unnamed x20 -> x22, local copies, waits for them, and re-layouts: 4.55 us -> 5.29 us
where the time goes in v4:
time: 113 us; the launch traced here: 112 us
  Pallas kernels  106 us (94%)
  local copies, waits for them, and re-layouts  5.29 us (5%)
    pallas_call x1, Pallas kernels, reduce_call(): pl.pallas_call(reduce_kernel, out_shape=(jax.ShapeDtypeStruct((TOK, 2048)...  54.9 us
    pallas_call x1, Pallas kernels, gather_call(): pl.pallas_call(gather_kernel, out_shape=(jax.ShapeDtypeStruct((2, WIDE, H...  39.5 us
    pallas_call x1, Pallas kernels, attend_call(): pl.pallas_call(attend_kernel, out_shape=(jax.ShapeDtypeStruct((512, 512),...  9.76 us
    unnamed x22, local copies, waits for them, and re-layouts  5.29 us

profile of v4, /device:TPU:1, one launch (start us, length us, event | category | flops | bytes accessed | tf_op | source)
XLA Modules:
  0.0 112.1 jit_solution(7153430245478367600)
XLA Ops:
  0.6 0.0 copy-start
  0.6 0.0 copy-start.1
  0.7 1.1 copy-done.1
  1.8 0.0 copy-start.2
  1.8 1.0 copy-done.2
  2.8 0.0 copy-start.3
  2.8 0.9 copy-done.3
  3.7 0.0 copy-start.4
  3.7 0.9 copy-done.4
  4.6 0.0 copy-start.9
  4.6 0.7 copy-done.9
  5.3 0.0 copy-start.5
  5.3 0.0 copy-start.6
  5.3 0.0 copy-start.7
  5.3 0.0 copy-start.8
  5.3 39.5 %gather.1 = (bf16[2,1024,128]{2,1,0:T(8,128)(2,1)S(1)}, bf16[512,512]{1,0:T(8,128)(2,1)S(1)}, bf16[4096,128]{1,0:T(8,128)(2,1)S(1)}, bf16[4096,128]{1,0:T(8,128)...) custom-call(s32[1,16]{1,0:T(1,128)S(1)} %copy-done.9, ...), custom_call_target="tpu_custom_call" | custom-call | tf_op jit(solution)/shard_map/gather/pallas_call | solution.py:259
  44.9 0.0 copy-start.10
  44.9 0.6 copy-done.10
  45.5 9.8 %attend.1 = (bf16[512,512]{1,0:T(8,128)(2,1)S(1)}, bf16[4096,128]{1,0:T(8,128)(2,1)S(1)}, bf16[4096,128]{1,0:T(8,128)(2,1)S(1)}) custom-call(s32[1,16]{1,0:T(1,128)S(1)} %copy-done.10, bf16[2,1024,128]{2,1,0:T(8,128)(2,1)S(1)} %get-tuple-element.30.q_ref, bf16[512,512]{1,0:T(8,128)(2,1)S(1)} %get-tuple-element.31.do_ref, ...), custom_call_target="tpu_custom_call" | custom-call | tf_op jit(solution)/shard_map/attend/pallas_call | solution.py:344
  55.3 0.0 copy-done
  55.3 0.0 copy-done.5
  55.3 0.0 copy-done.6
  55.3 0.0 copy-done.7
  55.3 0.0 copy-done.8
  55.3 54.9 %reduce.1 = (bf16[128,2048]{1,0:T(8,128)(2,1)S(1)}, bf16[128,512]{1,0:T(8,128)(2,1)S(1)}, bf16[128,512]{1,0:T(8,128)(2,1)S(1)}, bf16[2,2,8,16,384]{4,3,2,1,0:T(8,128)(2,1)S(1)}) custom-call(bf16[512,512]{1,0:T(8,128)(2,1)S(1)} %get-tuple-element.39.dq_ref, bf16[4096,128]{1,0:T(8,128)(2,1)S(1)} %get-tuple-element.40.dk_ref, ...), custom_call_target="tpu_custom_call" | custom-call | tf_op jit(solution)/shard_map/reduce/pallas_call | solution.py:556
  110.2 1.7 %finish.1 = (bf16[128,2048]{1,0:T(8,128)(2,1)}, bf16[128,512]{1,0:T(8,128)(2,1)}, bf16[128,512]{1,0:T(8,128)(2,1)}, f32[16,4096]{1,0:T(8,128)}, f32[16,2048]{1,0...) custom-call(bf16[128,2048]{1,0:T(8,128)(2,1)S(1)} %get-tuple-element.42.dql_ref, ...), custom_call_target="tpu_custom_call" | custom-call | tf_op jit(solution)/shard_map/finish/pallas_call | solution.py:605
Async XLA Ops:
  0.6 54.6 %copy-start = (bf16[1,128,4096]{2,1,0:T(8,128)(2,1)S(1)}, bf16[1,128,4096]{2,1,0:T(8,128)(2,1)}, u32[]{:S(2)}) copy-start(bf16[1,128,4096]{2,1,0:T(8,128)(2,1)} %param.14) | copy-start | bytes 3145732
  0.6 1.1 %copy-start.1 = (bf16[1,128,2048]{2,1,0:T(8,128)(2,1)S(1)}, bf16[1,128,2048]{2,1,0:T(8,128)(2,1)}, u32[]{:S(2)}) copy-start(bf16[1,128,2048]{2,1,0:T(8,128)(2,1)} %param.10) | copy-start | bytes 1572868
  1.8 1.0 copy-start.2
  2.8 0.9 copy-start.3
  3.7 0.9 copy-start.4
  4.6 0.7 copy-start.9
  5.3 50.0 %copy-start.5 = (bf16[16,4096]{1,0:T(8,128)(2,1)S(1)}, bf16[16,4096]{1,0:T(8,128)(2,1)}, u32[]{:S(2)}) copy-start(bf16[16,4096]{1,0:T(8,128)(2,1)} %qa_ref.1) | copy-start | bytes 393220
  5.3 50.0 %copy-start.6 = (bf16[16,4096]{1,0:T(8,128)(2,1)S(1)}, bf16[16,4096]{1,0:T(8,128)(2,1)}, u32[]{:S(2)}) copy-start(bf16[16,4096]{1,0:T(8,128)(2,1)} %va_ref.1) | copy-start | bytes 393220
  5.3 50.0 %copy-start.7 = (bf16[16,2048]{1,0:T(8,128)(2,1)S(1)}, bf16[16,2048]{1,0:T(8,128)(2,1)}, u32[]{:S(2)}) copy-start(bf16[16,2048]{1,0:T(8,128)(2,1)} %qb_ref.1) | copy-start | bytes 196612
  5.3 50.0 %copy-start.8 = (bf16[16,512]{1,0:T(8,128)(2,1)S(1)}, bf16[16,512]{1,0:T(8,128)(2,1)}, u32[]{:S(2)}) copy-start(bf16[16,512]{1,0:T(8,128)(2,1)} %vb_ref.1) | copy-start | bytes 49156
  44.9 0.7 copy-start.10

commit v5 on v4

--- a/solution.py
+++ b/solution.py
@@ -370,7 +370,8 @@
     own = 2 * a + c
     peers = group_peers(a, c)
     ways = (1, -1)
-    chunks = ((dv_ref, 1 - a), (dv_ref, a), (dk_ref, 1 - a), (dk_ref, a))
+    spots = ((1 - a, c), (1 - a, 1 - c), (a, 1 - c), (a, c))
+    chunks = tuple((ref, y, side) for ref in (dv_ref, dk_ref) for y, side in spots)
     head_cols = pl.ds(mult(own * HEAD, HEAD), HEAD)
     wide_cols = pl.ds(mult(own * 512, 512), 512)
     seat = lax.axis_index("dp") * 2 + a
@@ -394,11 +395,11 @@
         remote(dst, dst, ssem, rsem, to).wait_recv()
 
     def rows_of(j, dist):
-        y = chunks[j][1]
-        return pl.ds(mult(y * HALF_SEQ + ((z + 2 * RING + dist) % RING) * CHIP_ROWS, CHIP_ROWS), CHIP_ROWS)
+        _, y, side = chunks[j]
+        return pl.ds(mult(y * HALF_SEQ + ((z + 2 * RING + dist) % RING) * CHIP_ROWS + side * TOK, TOK), TOK)
 
     def at(w, d, j):
-        return (w * 4 + d - 1) * 4 + j
+        return (w * 4 + d - 1) * 8 + j
 
     def starts_far(w, j):
         return (j % 2 == 0) == (w == 0)
@@ -480,16 +481,15 @@
                 send_on(w, d, j, rb.at[slot])
 
     def last(i, dst):
-        for j in (2 * i, 2 * i + 1):
+        for k, p in enumerate((1, 2, 0, None)):
+            j = 4 * i + k
             for w in (0, 1):
                 arrived(w, 1, j)
             both = rb[at(0, 1, j)].astype(f32) + rb[at(1, 1, j)].astype(f32)
             fin[j] = (both + chunks[j][0][rows_of(j, 0), :].astype(f32)).astype(bf)
-            for p in ((1, 2) if j % 2 == 0 else (0,)):
-                go(fin.at[j, pl.ds(mult(peers[p][1] * TOK, TOK), TOK)], dst.at[:, head_cols],
-                   gs.at[2 * p + i], gr.at[2 * p + i], ids[p])
-        one = pltpu.make_async_copy(
-            fin.at[2 * i + 1, pl.ds(mult(c * TOK, TOK), TOK)], dst.at[:, head_cols], ls.at[1 + i])
+            if p is not None:
+                go(fin.at[j], dst.at[:, head_cols], gs.at[2 * p + i], gr.at[2 * p + i], ids[p])
+        one = pltpu.make_async_copy(fin.at[4 * i + 3], dst.at[:, head_cols], ls.at[1 + i])
         one.start()
         return one
 
@@ -499,7 +499,7 @@
             cols = pl.ds(mult((2 * pa + pc) * HEAD, HEAD), HEAD)
             came(dst.at[:, cols], gs.at[2 * p + i], gr.at[2 * p + i], ids[p])
 
-    values, keys = (0, 1), (2, 3)
+    values, keys = (0, 1, 2, 3), (4, 5, 6, 7)
     first_sends(values)
     for p, (pa, pc) in enumerate(peers):
         go(dq_ref.at[pl.ds(mult((2 * pa + pc) * TOK, TOK), TOK)], dql.at[:, wide_cols],
@@ -563,13 +563,13 @@
         in_specs=[VMEM] * 8,
         out_specs=(VMEM,) * 4,
         scratch_shapes=[
-            pltpu.VMEM((32, CHIP_ROWS, HEAD), bf), pltpu.VMEM((4, CHIP_ROWS, HEAD), bf),
+            pltpu.VMEM((64, TOK, HEAD), bf), pltpu.VMEM((8, TOK, HEAD), bf),
             pltpu.VMEM((TOK, 2048), bf), pltpu.VMEM((TOK, 512), bf), pltpu.VMEM((TOK, 512), bf),
             pltpu.VMEM((2, RANK, PACKED), bf), pltpu.VMEM((2, RANK, CORE_COLS), bf),
             pltpu.VMEM((2, RANK, CORE_COLS), bf), pltpu.VMEM((14, RANK, Z_COLS), bf),
             pltpu.VMEM((2, RANK, Z_COLS), bf), pltpu.VMEM((2, 16, RANK, Z_COLS), bf),
             pltpu.VMEM((2, 2, RING, RANK, Z_COLS), bf),
-            dma((6,)), dma((6,)), dma((3,)), dma((3,)), dma((32,)), dma((32,)), dma((3,)),
+            dma((6,)), dma((6,)), dma((3,)), dma((3,)), dma((64,)), dma((64,)), dma((3,)),
             dma((2,)), dma((2,)), dma((14,)), dma((14,)), dma((30,)), dma((30,)),
             dma((14,)), dma((14,)), dma((2,)), dma((2,)),
         ],

time: 113 us -> 111 us (0.982)
  Pallas kernels: 106 us -> 104 us
    pallas_call x1, Pallas kernels: 9.76 us -> 8.38 us  [attend_call(): pl.pallas_call(attend_kernel, out_shape=(jax.ShapeDtypeStruct((512, 512),...]
where the time goes in v5:
time: 111 us; the launch traced here: 110 us
  Pallas kernels  104 us (94%)
  local copies, waits for them, and re-layouts  5.29 us (5%)
    pallas_call x1, Pallas kernels, reduce_call(): pl.pallas_call(reduce_kernel, out_shape=(jax.ShapeDtypeStruct((TOK, 2048)...  54.3 us
    pallas_call x1, Pallas kernels, gather_call(): pl.pallas_call(gather_kernel, out_shape=(jax.ShapeDtypeStruct((2, WIDE, H...  39.5 us
    pallas_call x1, Pallas kernels, attend_call(): pl.pallas_call(attend_kernel, out_shape=(jax.ShapeDtypeStruct((512, 512),...  8.38 us
    unnamed x22, local copies, waits for them, and re-layouts  5.29 us

profile of v5, /device:TPU:1, one launch (start us, length us, event | category | flops | bytes accessed | tf_op | source)
XLA Modules:
  0.0 110.2 jit_solution(6011416119036292973)
XLA Ops:
  0.6 0.0 copy-start
  0.6 0.0 copy-start.1
  0.7 1.1 %copy-done.1 = bf16[1,128,2048]{2,1,0:T(8,128)(2,1)S(1)} copy-done((bf16[1,128,2048]{2,1,0:T(8,128)(2,1)S(1)}, bf16[1,128,2048]{2,1,0:T(8,128)(2,1)}, u32[]{:S(2)}) %copy-start.1) | copy-done | bytes 524312
  1.8 0.0 copy-start.2
  1.8 1.0 copy-done.2
  2.8 0.0 copy-start.3
  2.8 0.9 copy-done.3
  3.7 0.0 copy-start.4
  3.7 0.9 copy-done.4
  4.6 0.0 copy-start.9
  4.6 0.7 copy-done.9
  5.3 0.0 copy-start.5
  5.3 0.0 copy-start.6
  5.3 0.0 copy-start.7
  5.3 0.0 copy-start.8
  5.3 39.5 %gather.1 = (bf16[2,1024,128]{2,1,0:T(8,128)(2,1)S(1)}, bf16[512,512]{1,0:T(8,128)(2,1)S(1)}, bf16[4096,128]{1,0:T(8,128)(2,1)S(1)}, bf16[4096,128]{1,0:T(8,128)...) custom-call(s32[1,16]{1,0:T(1,128)S(1)} %copy-done.9, ...), custom_call_target="tpu_custom_call" | custom-call | tf_op jit(solution)/shard_map/gather/pallas_call | solution.py:259
  44.9 0.0 copy-start.10
  44.9 0.6 copy-done.10
  45.5 8.4 %attend.1 = (bf16[512,512]{1,0:T(8,128)(2,1)S(1)}, bf16[4096,128]{1,0:T(8,128)(2,1)S(1)}, bf16[4096,128]{1,0:T(8,128)(2,1)S(1)}) custom-call(s32[1,16]{1,0:T(1,128)S(1)} %copy-done.10, bf16[2,1024,128]{2,1,0:T(8,128)(2,1)S(1)} %get-tuple-element.30.q_ref, bf16[512,512]{1,0:T(8,128)(2,1)S(1)} %get-tuple-element.31.do_ref, ...), custom_call_target="tpu_custom_call" | custom-call | tf_op jit(solution)/shard_map/attend/pallas_call | solution.py:344
  53.9 0.0 copy-done
  53.9 0.0 copy-done.5
  53.9 0.0 copy-done.6
  53.9 0.0 copy-done.7
  53.9 0.0 copy-done.8
  53.9 54.3 %reduce.1 = (bf16[128,2048]{1,0:T(8,128)(2,1)S(1)}, bf16[128,512]{1,0:T(8,128)(2,1)S(1)}, bf16[128,512]{1,0:T(8,128)(2,1)S(1)}, bf16[2,2,8,16,384]{4,3,2,1,0:T(8,128)(2,1)S(1)}) custom-call(bf16[512,512]{1,0:T(8,128)(2,1)S(1)} %get-tuple-element.39.dq_ref, bf16[4096,128]{1,0:T(8,128)(2,1)S(1)} %get-tuple-element.40.dk_ref, ...), custom_call_target="tpu_custom_call" | custom-call | tf_op jit(solution)/shard_map/reduce/pallas_call | solution.py:556
  108.3 1.7 %finish.1 = (bf16[128,2048]{1,0:T(8,128)(2,1)}, bf16[128,512]{1,0:T(8,128)(2,1)}, bf16[128,512]{1,0:T(8,128)(2,1)}, f32[16,4096]{1,0:T(8,128)}, f32[16,2048]{1,0...) custom-call(bf16[128,2048]{1,0:T(8,128)(2,1)S(1)} %get-tuple-element.42.dql_ref, ...), custom_call_target="tpu_custom_call" | custom-call | tf_op jit(solution)/shard_map/finish/pallas_call | solution.py:605
Async XLA Ops:
  0.6 53.3 %copy-start = (bf16[1,128,4096]{2,1,0:T(8,128)(2,1)S(1)}, bf16[1,128,4096]{2,1,0:T(8,128)(2,1)}, u32[]{:S(2)}) copy-start(bf16[1,128,4096]{2,1,0:T(8,128)(2,1)} %param.14) | copy-start | bytes 3145732
  0.6 1.1 %copy-start.1 = (bf16[1,128,2048]{2,1,0:T(8,128)(2,1)S(1)}, bf16[1,128,2048]{2,1,0:T(8,128)(2,1)}, u32[]{:S(2)}) copy-start(bf16[1,128,2048]{2,1,0:T(8,128)(2,1)} %param.10) | copy-start | bytes 1572868
  1.8 1.0 copy-start.2
  2.8 0.9 copy-start.3
  3.7 0.9 copy-start.4
  4.6 0.7 copy-start.9
  5.3 48.6 %copy-start.5 = (bf16[16,4096]{1,0:T(8,128)(2,1)S(1)}, bf16[16,4096]{1,0:T(8,128)(2,1)}, u32[]{:S(2)}) copy-start(bf16[16,4096]{1,0:T(8,128)(2,1)} %qa_ref.1) | copy-start | bytes 393220
  5.3 48.6 %copy-start.6 = (bf16[16,4096]{1,0:T(8,128)(2,1)S(1)}, bf16[16,4096]{1,0:T(8,128)(2,1)}, u32[]{:S(2)}) copy-start(bf16[16,4096]{1,0:T(8,128)(2,1)} %va_ref.1) | copy-start | bytes 393220
  5.3 48.6 %copy-start.7 = (bf16[16,2048]{1,0:T(8,128)(2,1)S(1)}, bf16[16,2048]{1,0:T(8,128)(2,1)}, u32[]{:S(2)}) copy-start(bf16[16,2048]{1,0:T(8,128)(2,1)} %qb_ref.1) | copy-start | bytes 196612
  5.3 48.7 %copy-start.8 = (bf16[16,512]{1,0:T(8,128)(2,1)S(1)}, bf16[16,512]{1,0:T(8,128)(2,1)}, u32[]{:S(2)}) copy-start(bf16[16,512]{1,0:T(8,128)(2,1)} %vb_ref.1) | copy-start | bytes 49156
  44.9 0.7 copy-start.10

commit v6 on v5

--- a/solution.py
+++ b/solution.py
@@ -242,13 +242,14 @@
         for w in (0, 1):
             fold_both(1 - a if half else a, 0, w)
         relay(1, half)
-    for s in (2, 3):
-        for half in (0, 1):
-            relay(s, half)
+    for half in (0, 1):
+        relay(2, half)
+    crossed(1, doall)
+    dog_ref[...] = doall[...]
+    for half in (0, 1):
+        relay(3, half)
     kg_ref[...] = kall[...]
     vg_ref[...] = vall[...]
-    crossed(1, doall)
-    dog_ref[...] = doall[...]
     for one in sent:
         one.wait_send()
 
@@ -523,13 +524,13 @@
     part[0, :, 0:4096] = (2.0 * nn(query_low, hidden)).astype(bf)
     core_send(0)
     forward(3, keys)
+    z_send(0)
     returned(0, dvl, own_values)
     value = dvl[...]
     part[1, :, 4096:4608] = (2.0 * nn(value_proj, value)).astype(bf)
     value_low = nt(vb_ref[...], value).astype(bf)
     part[1, :, 0:4096] = (2.0 * nn(value_low, hidden)).astype(bf)
     core_send(1)
-    z_send(0)
     z_send(1)
     forward(2, keys)
     seat_send(0)

time: 111 us -> 111 us (level)
    pallas_call x1, Pallas kernels: 54.3 us -> 56.4 us  [reduce_call(): pl.pallas_call(reduce_kernel, out_shape=(jax.ShapeDtypeStruct((TOK, 2048)...]
    pallas_call x1, Pallas kernels: 8.38 us -> 7 us  [attend_call(): pl.pallas_call(attend_kernel, out_shape=(jax.ShapeDtypeStruct((512, 512),...]
where the time goes in v6:
time: 111 us
  Pallas kernels  105 us (95%)
  local copies, waits for them, and re-layouts  5.29 us (5%)
    pallas_call x1, Pallas kernels, reduce_call(): pl.pallas_call(reduce_kernel, out_shape=(jax.ShapeDtypeStruct((TOK, 2048)...  56.4 us
    pallas_call x1, Pallas kernels, gather_call(): pl.pallas_call(gather_kernel, out_shape=(jax.ShapeDtypeStruct((2, WIDE, H...  39.5 us
    pallas_call x1, Pallas kernels, attend_call(): pl.pallas_call(attend_kernel, out_shape=(jax.ShapeDtypeStruct((512, 512),...  7 us
    unnamed x22, local copies, waits for them, and re-layouts  5.29 us

profile of v6, /device:TPU:1, one launch (start us, length us, event | category | flops | bytes accessed | tf_op | source)
XLA Modules:
  0.0 110.8 jit_solution(17094272953076019060)
XLA Ops:
  0.6 0.0 copy-start
  0.6 0.0 copy-start.1
  0.7 1.1 %copy-done.1 = bf16[1,128,2048]{2,1,0:T(8,128)(2,1)S(1)} copy-done((bf16[1,128,2048]{2,1,0:T(8,128)(2,1)S(1)}, bf16[1,128,2048]{2,1,0:T(8,128)(2,1)}, u32[]{:S(2)}) %copy-start.1) | copy-done | bytes 524312
  1.8 0.0 copy-start.2
  1.8 1.0 copy-done.2
  2.8 0.0 copy-start.3
  2.8 0.9 copy-done.3
  3.7 0.0 copy-start.4
  3.7 0.9 copy-done.4
  4.6 0.0 copy-start.9
  4.6 0.7 copy-done.9
  5.3 0.0 copy-start.5
  5.3 0.0 copy-start.6
  5.3 0.0 copy-start.7
  5.3 0.0 copy-start.8
  5.3 39.5 %gather.1 = (bf16[2,1024,128]{2,1,0:T(8,128)(2,1)S(1)}, bf16[512,512]{1,0:T(8,128)(2,1)S(1)}, bf16[4096,128]{1,0:T(8,128)(2,1)S(1)}, bf16[4096,128]{1,0:T(8,128)...) custom-call(s32[1,16]{1,0:T(1,128)S(1)} %copy-done.9, ...), custom_call_target="tpu_custom_call" | custom-call | tf_op jit(solution)/shard_map/gather/pallas_call | solution.py:260
  44.8 0.0 copy-start.10
  44.8 0.6 copy-done.10
  45.5 7.0 %attend.1 = (bf16[512,512]{1,0:T(8,128)(2,1)S(1)}, bf16[4096,128]{1,0:T(8,128)(2,1)S(1)}, bf16[4096,128]{1,0:T(8,128)(2,1)S(1)}) custom-call(s32[1,16]{1,0:T(1,128)S(1)} %copy-done.10, bf16[2,1024,128]{2,1,0:T(8,128)(2,1)S(1)} %get-tuple-element.30.q_ref, bf16[512,512]{1,0:T(8,128)(2,1)S(1)} %get-tuple-element.31.do_ref, ...), custom_call_target="tpu_custom_call" | custom-call | tf_op jit(solution)/shard_map/attend/pallas_call | solution.py:345
  52.5 0.0 copy-done
  52.5 0.0 copy-done.5
  52.5 0.0 copy-done.6
  52.5 0.0 copy-done.7
  52.5 0.0 copy-done.8
  52.5 56.4 %reduce.1 = (bf16[128,2048]{1,0:T(8,128)(2,1)S(1)}, bf16[128,512]{1,0:T(8,128)(2,1)S(1)}, bf16[128,512]{1,0:T(8,128)(2,1)S(1)}, bf16[2,2,8,16,384]{4,3,2,1,0:T(8,128)(2,1)S(1)}) custom-call(bf16[512,512]{1,0:T(8,128)(2,1)S(1)} %get-tuple-element.39.dq_ref, bf16[4096,128]{1,0:T(8,128)(2,1)S(1)} %get-tuple-element.40.dk_ref, ...), custom_call_target="tpu_custom_call" | custom-call | tf_op jit(solution)/shard_map/reduce/pallas_call | solution.py:557
  108.9 1.7 %finish.1 = (bf16[128,2048]{1,0:T(8,128)(2,1)}, bf16[128,512]{1,0:T(8,128)(2,1)}, bf16[128,512]{1,0:T(8,128)(2,1)}, f32[16,4096]{1,0:T(8,128)}, f32[16,2048]{1,0...) custom-call(bf16[128,2048]{1,0:T(8,128)(2,1)S(1)} %get-tuple-element.42.dql_ref, ...), custom_call_target="tpu_custom_call" | custom-call | tf_op jit(solution)/shard_map/finish/pallas_call | solution.py:606
Async XLA Ops:
  0.6 51.8 %copy-start = (bf16[1,128,4096]{2,1,0:T(8,128)(2,1)S(1)}, bf16[1,128,4096]{2,1,0:T(8,128)(2,1)}, u32[]{:S(2)}) copy-start(bf16[1,128,4096]{2,1,0:T(8,128)(2,1)} %param.14) | copy-start | bytes 3145732
  0.6 1.1 %copy-start.1 = (bf16[1,128,2048]{2,1,0:T(8,128)(2,1)S(1)}, bf16[1,128,2048]{2,1,0:T(8,128)(2,1)}, u32[]{:S(2)}) copy-start(bf16[1,128,2048]{2,1,0:T(8,128)(2,1)} %param.10) | copy-start | bytes 1572868
  1.8 1.0 copy-start.2
  2.8 0.9 copy-start.3
  3.7 0.9 copy-start.4
  4.6 0.7 copy-start.9
  5.3 47.2 %copy-start.5 = (bf16[16,4096]{1,0:T(8,128)(2,1)S(1)}, bf16[16,4096]{1,0:T(8,128)(2,1)}, u32[]{:S(2)}) copy-start(bf16[16,4096]{1,0:T(8,128)(2,1)} %qa_ref.1) | copy-start | bytes 393220
  5.3 47.2 %copy-start.6 = (bf16[16,4096]{1,0:T(8,128)(2,1)S(1)}, bf16[16,4096]{1,0:T(8,128)(2,1)}, u32[]{:S(2)}) copy-start(bf16[16,4096]{1,0:T(8,128)(2,1)} %va_ref.1) | copy-start | bytes 393220
  5.3 47.2 %copy-start.7 = (bf16[16,2048]{1,0:T(8,128)(2,1)S(1)}, bf16[16,2048]{1,0:T(8,128)(2,1)}, u32[]{:S(2)}) copy-start(bf16[16,2048]{1,0:T(8,128)(2,1)} %qb_ref.1) | copy-start | bytes 196612
  5.3 47.2 %copy-start.8 = (bf16[16,512]{1,0:T(8,128)(2,1)S(1)}, bf16[16,512]{1,0:T(8,128)(2,1)}, u32[]{:S(2)}) copy-start(bf16[16,512]{1,0:T(8,128)(2,1)} %vb_ref.1) | copy-start | bytes 49156
  44.8 0.7 copy-start.10
